TPU v7x, 256 devices: a whole 4x4x8 slice. The times are simulated.
256 devices in a mesh: expert: 32 (over z, x_lo, core), tensor: 8 (over y, x_hi).
Axes of the slice: x: 4 (x_hi: 2, x_lo: 2; x = x_hi * 2 + x_lo), y: 4, z: 8, core: 2. Of those that a mesh axis runs over, the one named last changes fastest.
Arguments:
- tokens: bfloat16 [2048, 2048], P('expert'), may hold values from -6 to 6
- expert_ids: int32 [2048, 6], replicated, may hold values from 0 to 63, all different within a row; in each aligned block of 2048 rows (0 to 2047, 2048 to 4095, ...) at most 256 rows name the same one
- gate_probs: float32 [2048, 6], replicated, may hold values from 0.02 to 0.6
- w_gate: bfloat16 [64, 2048, 1408], P('expert', None, 'tensor'), may hold values from -0.125 to 0.125
- w_up: bfloat16 [64, 2048, 1408], P('expert', None, 'tensor'), may hold values from -0.125 to 0.125
- w_down: bfloat16 [64, 1408, 2048], P('expert', 'tensor'), may hold values from -0.15625 to 0.15625
- shared_gate: bfloat16 [2048, 2816], P(None, 'tensor'), may hold values from -0.125 to 0.125
- shared_up: bfloat16 [2048, 2816], P(None, 'tensor'), may hold values from -0.125 to 0.125
- shared_down: bfloat16 [2816, 2048], P('tensor'), may hold values from -0.109375 to 0.109375
Outputs:
- layer_out: bfloat16 [2048, 2048], P('expert')
Inputs may be any that keep to these rules, and one draw needn't show every extreme that they name: `expert_ids`: each row names 6 different experts. Over all 2048 tokens no expert is named more than 256 times, a bound that some block reaches.
All inputs are finite; a program needn't handle non-finite values.
Results may differ from a plain program's by a relative error of at most 0.011.
Values may be sent and summed in bfloat16 or wider, within the bound.
A program may use at most 64 MiB of HBM per device.

v0:
```python
import math

import jax
import jax.numpy as jnp
from jax import lax
from jax.sharding import Mesh
from jax.sharding import PartitionSpec as P

TENSOR = ("tensor_0", "tensor_1")


def scatter_axes(x, axes, dim):
    if not axes:
        return x
    nearer = lax.psum_scatter(x, axes[0], scatter_dimension=dim, tiled=True)
    return scatter_axes(nearer, axes[1:], dim)


def cut_along(x, dim, size):
    dims = x.shape
    blocks = x.reshape(*dims[:dim], size, dims[dim] // size, *dims[dim + 1 :])
    return jnp.moveaxis(blocks, dim, 0)


def sent_and_summed(x, axis, dim):
    size = lax.axis_size(axis)
    blocks = lax.all_to_all(cut_along(x, dim, size), axis, 0, 0, tiled=True)
    return jnp.sum(blocks.astype(jnp.float32), axis=0)


def summed_on_arrival(x, axis, dim):
    blocks = cut_along(x, dim, lax.axis_size(axis))
    arrived = lax.all_to_all(blocks, axis, split_axis=0, concat_axis=0, tiled=True)
    return arrived.sum(axis=0)


def sent_to_all(x, axis):
    copies = jnp.broadcast_to(x, (lax.axis_size(axis), *x.shape))
    return lax.all_to_all(copies, axis, split_axis=0, concat_axis=0, tiled=True)


def laid_out(blocks, dim):
    blocks = jnp.moveaxis(blocks, 0, dim)
    dims = blocks.shape
    return blocks.reshape(*dims[:dim], dims[dim] * dims[dim + 1], *dims[dim + 2 :])


def collect(x, axis, dim):
    blocks = sent_to_all(x, axis)
    return laid_out(blocks, dim)


def place_rows(expert_ids, gate_probs, expert):
    hits = expert_ids == expert
    row_hit = jnp.sum(hits.astype(jnp.float32), axis=1)
    total_rows = row_hit.shape[0]
    block = math.gcd(total_rows, 128)
    blocks = row_hit.reshape(total_rows // block, block)
    lower = jnp.arange(block, dtype=jnp.int32)
    strict = (lower[:, None] < lower[None, :]).astype(jnp.float32)
    inside = jnp.dot(blocks, strict, precision=lax.Precision.HIGHEST)
    sums = jnp.sum(blocks, axis=1)
    offsets = jnp.cumsum(sums) - sums
    before = (inside + offsets[:, None]).reshape(total_rows)
    target = jnp.where(row_hit > 0.5, before, -1.0).astype(jnp.int32)
    weight = jnp.sum(jnp.where(hits, gate_probs, 0.0), axis=1)
    return (target, weight)


def body(tokens, expert_ids, gate_probs, w_gate, w_up, w_down, shared_gate, shared_up, shared_down):
    local_count = w_gate.shape[0]
    own_rows = tokens.shape[0]
    capacity = 4 * own_rows
    first_expert = lax.axis_index("expert") * local_count
    local_experts = first_expert + jnp.arange(local_count, dtype=jnp.int32)
    targets, weights = jax.vmap(lambda expert: place_rows(expert_ids, gate_probs, expert))(
        local_experts
    )
    positions = jnp.arange(capacity, dtype=jnp.int32)
    columns = targets
    picker = (positions[None, :, None] == columns[:, None, :]).astype(jnp.bfloat16)
    collected = jnp.einsum(
        "lcr,rd->lcd",
        picker,
        lax.all_gather(tokens, "expert", axis=0, tiled=True),
        preferred_element_type=jnp.float32,
    )
    dispatched = collected.astype(jnp.bfloat16)
    gate = jnp.einsum("lcd,ldf->lcf", dispatched, w_gate, preferred_element_type=jnp.float32)
    upper = jnp.einsum("lcd,ldf->lcf", dispatched, w_up, preferred_element_type=jnp.float32)
    hidden = (jax.nn.silu(gate) * upper).astype(jnp.bfloat16)
    partial_value = jnp.einsum("lcf,lfd->lcd", hidden, w_down, preferred_element_type=jnp.float32)
    sgate = jnp.dot(tokens, shared_gate, preferred_element_type=jnp.float32)
    supper = jnp.dot(tokens, shared_up, preferred_element_type=jnp.float32)
    shared_hidden = (jax.nn.silu(sgate) * supper).astype(jnp.bfloat16)
    shared_part = jnp.dot(shared_hidden, shared_down, preferred_element_type=jnp.float32)
    width_sum = scatter_axes(partial_value.astype(jnp.bfloat16), TENSOR, 2).astype(jnp.float32)
    high_part = width_sum.astype(jnp.bfloat16)
    low_part = (width_sum - high_part.astype(jnp.float32)).astype(jnp.bfloat16)
    columns = targets
    picker = (columns[:, :, None] == positions[None, None, :]).astype(jnp.bfloat16)
    picked = jnp.einsum("lrc,lcd->lrd", picker, high_part, preferred_element_type=jnp.float32)
    picked = picked + jnp.einsum(
        "lrc,lcd->lrd", picker, low_part, preferred_element_type=jnp.float32
    )
    factor = jnp.where(columns >= 0, weights, 0.0)
    routed = sent_and_summed(
        jnp.sum(factor[:, :, None] * picked, axis=0).astype(jnp.bfloat16), "expert", 0
    )
    shared = summed_on_arrival(shared_part, TENSOR, 1)
    mixed = (shared + routed).astype(jnp.bfloat16)
    return collect(mixed, TENSOR, 1)


def solution(mesh):
    torus = Mesh(
        mesh.devices.reshape(mesh.shape["expert"], 4, 2), ("expert", "tensor_0", "tensor_1")
    )
    return jax.shard_map(
        body,
        mesh=torus,
        in_specs=(
            P("expert", None),
            P(),
            P(),
            P("expert", None, TENSOR),
            P("expert", None, TENSOR),
            P("expert", TENSOR, None),
            P(None, TENSOR),
            P(None, TENSOR),
            P(TENSOR, None),
        ),
        out_specs=P("expert", None),
        check_vma=False,
    )
```

profile of v0, /device:TPU:2, one launch (start us, length us, event | category | flops | bytes accessed | tf_op | source)
XLA Modules:
  0.0 217.5 jit_solution(11732188097267860103)
XLA Ops:
  6.5 0.0 copy-start
  6.5 0.0 all-gather.2.cloned.1.call-start
  6.5 0.7 all-gather.2.cloned.1.call-update
  7.3 0.0 reduce-scatter.3.cloned.1.call-start
  7.3 1.1 fusion.21
  8.4 0.1 bitcast_reduce_fusion
  8.5 0.2 reduce_window_sum.11
  8.7 0.1 fusion.13
  8.8 0.7 compare_select_fusion.1
  9.5 74.2 %all-gather.2.cloned.1.call-done = bf16[2048,2048]{1,0:T(8,128)(2,1)} async-done(((bf16[64,2048]{1,0:T(8,128)(2,1)}), bf16[2048,2048]{1,0:T(8,128)(2,1)}) %all-gather.2.cloned.1.call-update) | async-done | bytes 8388624 | tf_op jit(solution)/shard_map/all_gather | solution.py:85
  83.7 0.0 copy-start.3
  83.7 8.2 %fusion.4 = bf16[2,256,2048]{2,1,0:T(8,128)(2,1)S(1)} fusion(bf16[2048,2048]{1,0:T(8,128)(2,1)} %all-gather.2.cloned.1.call-done, s32[2,2048]{1,0:T(2,128)S(1)} %get-tuple-element.8), kind=kOutput, calls=%fused_computation.8 | convolution fusion | flops 4297064448 | bytes 10502144 | tf_op jit(solution)/shard_map/lcr,rd->lcd/dot_general | solution.py:82
  91.9 0.0 copy-done.3
  91.9 1.6 fusion.37
  93.5 0.0 copy-done
  93.5 4.4 %convolution_convert_fusion = bf16[2,256,2048]{2,1,0:T(8,128)(2,1)} fusion(bf16[2,176,2048]{2,1,0:T(8,128)(2,1)S(1)} %copy-done, bf16[2,256,2048]{2,1,0:T(8,128)(2,1)S(1)} %fusion.4, bf16[2,2048,176]{1,2,0:T(8,128)(2,1)} %param.13, f32[2,256,176]{1,2,0:T(8,128)} %fusion.37), kind=kOutput, calls=%fused_computation.7 | convolution fusion | flops 739786752 | bytes 7438336 | tf_op jit(solution)/shard_map/lcf,lfd->lcd/dot_general | solution.py:92
  97.9 0.0 copy-start.1
  97.9 0.0 copy-start.2
  97.9 0.0 reduce-scatter.3.cloned.1.call-update
  97.9 0.0 reduce-scatter.5.cloned.1.call-start
  98.0 31.8 %reduce-scatter.3.cloned.1.call-done = bf16[2,256,512]{2,1,0:T(8,128)(2,1)} async-done(((bf16[2,256,2048]{2,1,0:T(8,128)(2,1)}), bf16[2,256,512]{2,1,0:T(8,128)(2,1)}) %reduce-scatter.3.cloned.1.call-update) | async-done | bytes 524304 | tf_op jit(solution)/shard_map/reduce_scatter | solution.py:15
  129.7 0.0 reduce-scatter.5.cloned.1.call-update
  129.8 0.0 copy-done.1
  129.8 0.0 copy-done.2
  129.8 0.6 fusion.36
  130.4 3.0 %fusion.12 = f32[64,2048]{1,0:T(8,128)S(1)} fusion(bf16[352,2048]{1,0:T(8,128)(2,1)} %param.17, bf16[64,2048]{1,0:T(8,128)(2,1)S(1)} %copy-done.1, bf16[2048,352]{0,1:T(8,128)(2,1)} %param.16, f32[64,352]{1,0:T(8,128)S(1)} %fusion.36), kind=kOutput, calls=%fused_computation.17 | convolution fusion | flops 184684544 | bytes 3760128 | tf_op jit(solution)/shard_map/dot_general | solution.py:96
  133.3 0.9 copy.33
  134.2 4.3 %all-to-all-start = ((f32[8,64,256]{2,1,0:T(8,128)}), f32[8,64,256]{2,1,0:T(8,128)S(1)}, u32[]{:S(2)}, u32[]{:S(2)}) async-start(f32[8,64,256]{2,1,0:T(8,128)} %bitcast.39), calls=%async_computation | async-start | bytes 1048576 | tf_op jit(solution)/shard_map/all_to_all | solution.py:33
  138.5 0.0 copy-start.5
  138.5 16.1 %reduce-scatter.5.cloned.1.call-done = bf16[2,256,256]{2,1,0:T(8,128)(2,1)} async-done(((bf16[2,256,512]{2,1,0:T(8,128)(2,1)}), bf16[2,256,256]{2,1,0:T(8,128)(2,1)}) %reduce-scatter.5.cloned.1.call-update) | async-done | bytes 262160 | tf_op jit(solution)/shard_map/reduce_scatter | solution.py:15
  154.6 0.0 copy-start.4
  154.6 2.0 fusion.2
  156.6 0.0 copy-done.5
  156.6 0.0 copy-done.4
  156.6 3.0 %multiply_reduce_fusion = bf16[2048,256]{1,0:T(8,128)(2,1)} fusion(f32[2,2048,256]{2,1,0:T(8,128)S(1)} %fusion.2, f32[2,2048]{1,0:T(2,128)S(1)} %copy-done.5, bf16[2,256,256]{2,1,0:T(8,128)(2,1)S(1)} %copy-done.4, s32[2,2048]{1,0:T(2,128)S(1)} %get-tuple-element.8), kind=kOutput, calls=%fused_computation.2 | convolution fusion | flops 540540928 | bytes 5537792 | tf_op jit(solution)/shard_map/lrc,lcd->lrd/dot_general | solution.py:102
  159.7 0.0 all-to-all-done
  159.7 8.6 %all-to-all-start.1 = ((bf16[32,64,256]{2,1,0:T(8,128)(2,1)}), bf16[32,64,256]{2,1,0:T(8,128)(2,1)S(1)}, u32[]{:S(2)}, u32[]{:S(2)}) async-start(bf16[32,64,256]{2,1,0:T(8,128)(2,1)} %bitcast.41), calls=%async_computation.3 | async-start | bytes 2097152 | tf_op jit(solution)/shard_map/all_to_all | solution.py:27
  168.4 28.9 %all-to-all-done.1 = bf16[32,64,256]{2,1,0:T(8,128)(2,1)S(1)} async-done(((bf16[32,64,256]{2,1,0:T(8,128)(2,1)}), bf16[32,64,256]{2,1,0:T(8,128)(2,1)S(1)}, u32[]{:S(2)}, u32[]{:S(2)}) %all-to-all-start.1) | async-done | bytes 1048608 | tf_op jit(solution)/shard_map/all_to_all | solution.py:27
  197.2 0.2 convert_reduce_fusion
  197.4 12.8 %all_to_all.15 = bf16[8,64,256]{2,1,0:T(8,128)(2,1)S(1)} all-to-all(bf16[8,64,256]{2,1,0:T(8,128)(2,1)S(1)} %broadcast_in_dim.33), channel_id=1, replica_groups=mesh['expert'=32,'tensor_0'=4,'tensor_1'=2] {'tensor_0','tensor_1'}, dimensions={0} | all-to-all | bytes 524288 | tf_op jit(solution)/shard_map/all_to_all | solution.py:39
  210.2 0.7 copy.22
  (5 shorter events, 0.1 us)
Async XLA Ops:
  6.5 87.0 %copy-start = (bf16[2,176,2048]{2,1,0:T(8,128)(2,1)S(1)}, bf16[2,176,2048]{2,1,0:T(8,128)(2,1)}, u32[]{:S(2)}) copy-start(bf16[2,176,2048]{2,1,0:T(8,128)(2,1)} %param.14) | copy-start | bytes 4325380
  6.5 77.2 %all-gather.2.cloned.1.call-start = ((), (), s32[]{:S(2)}) async-start(), calls=%async_computation.5 | async-start | bytes 8650752 | tf_op jit(solution)/shard_map/all_gather | solution.py:85
  7.3 122.5 %reduce-scatter.3.cloned.1.call-start = ((), (), s32[]{:S(2)}) async-start(), calls=%async_computation.6 | async-start | bytes 2621440 | tf_op jit(solution)/shard_map/reduce_scatter | solution.py:15
  83.7 8.2 %copy-start.3 = (bf16[2,2048,176]{1,2,0:T(8,128)(2,1)S(1)}, bf16[2,2048,176]{1,2,0:T(8,128)(2,1)}, u32[]{:S(2)}) copy-start(bf16[2,2048,176]{1,2,0:T(8,128)(2,1)} %param.12) | copy-start | bytes 4325380
  97.9 31.9 %copy-start.1 = (bf16[64,2048]{1,0:T(8,128)(2,1)S(1)}, bf16[64,2048]{1,0:T(8,128)(2,1)}, u32[]{:S(2)}) copy-start(bf16[64,2048]{1,0:T(8,128)(2,1)} %param.9) | copy-start | bytes 786436
  97.9 31.9 %copy-start.2 = (bf16[2048,352]{0,1:T(8,128)(2,1)S(1)}, bf16[2048,352]{0,1:T(8,128)(2,1)}, u32[]{:S(2)}) copy-start(bf16[2048,352]{0,1:T(8,128)(2,1)} %param.15) | copy-start | bytes 4325380
  97.9 56.7 %reduce-scatter.5.cloned.1.call-start = ((), (), s32[]{:S(2)}) async-start(), calls=%async_computation.7 | async-start | bytes 786432 | tf_op jit(solution)/shard_map/reduce_scatter | solution.py:15
  134.2 25.5 %all-to-all-start = ((f32[8,64,256]{2,1,0:T(8,128)}), f32[8,64,256]{2,1,0:T(8,128)S(1)}, u32[]{:S(2)}, u32[]{:S(2)}) async-start(f32[8,64,256]{2,1,0:T(8,128)} %bitcast.39), calls=%async_computation | async-start | bytes 1048576 | tf_op jit(solution)/shard_map/all_to_all | solution.py:33
  138.5 18.1 %copy-start.5 = (f32[2,2048]{1,0:T(2,128)S(1)}, f32[2,2048]{1,0:T(2,128)}, u32[]{:S(2)}) copy-start(f32[2,2048]{1,0:T(2,128)} %get-tuple-element.7) | copy-start | bytes 49156
  154.6 2.0 copy-start.4
  159.7 37.5 %all-to-all-start.1 = ((bf16[32,64,256]{2,1,0:T(8,128)(2,1)}), bf16[32,64,256]{2,1,0:T(8,128)(2,1)S(1)}, u32[]{:S(2)}, u32[]{:S(2)}) async-start(bf16[32,64,256]{2,1,0:T(8,128)(2,1)} %bitcast.41), calls=%async_computation.3 | async-start | bytes 2097152 | tf_op jit(solution)/shard_map/all_to_all | solution.py:27
Sparse Core Ops, SparseCore 0:
  9.2 74.4 all-gather.1
  98.0 31.6 reduce-scatter.2
  132.2 22.3 reduce-scatter.4
where the time goes:
time: 218 us; the launch traced here: 217 us
  waiting for transfers between devices  152 us (70%)
  matrix products  22.9 us (11%)
  between operations  13.2 us (6%)
  starting transfers between devices  13 us (6%)
  blocking collectives  12.8 us (6%)
  other arithmetic  2.23 us (1%)
    all_gather x1, waiting for transfers between devices, body(): lax.all_gather(tokens, 'expert', axis=0, tiled=True)  74.2 us
    reduce_scatter x2, waiting for transfers between devices, scatter_axes(): nearer = lax.psum_scatter(x, axes[0], scatter_dimension=dim, tiled=True)  47.9 us
    all_to_all x1, waiting for transfers between devices, sent_and_summed(): blocks = lax.all_to_all(cut_along(x, dim, size), axis, 0, 0, tiled=True)  28.9 us
    all_to_all x1, blocking collectives, sent_to_all(): return lax.all_to_all(copies, axis, split_axis=0, concat_axis=0, tiled=True)  12.8 us
    all_to_all x1, starting transfers between devices, sent_and_summed(): blocks = lax.all_to_all(cut_along(x, dim, size), axis, 0, 0, tiled=True)  8.63 us
    dot_general x1, matrix products, body(): jnp.einsum('lcr,rd->lcd', picker, lax.all_gather(tokens, 'expert', axis=0...  8.18 us
    dot_general x1, matrix products, body(): jnp.einsum('lcf,lfd->lcd', hidden, w_down, preferred_element_type=jnp.flo...  4.37 us
  transfers between devices with their start and end apart: 5, of which 4 were waited for; matrix products, arithmetic and copies ran while one was open for 5% of the time, Pallas kernels for 0%

commit v1 on v0

v1 whole, which is shorter than its diff:
```python
import jax
import jax.numpy as jnp
from jax import lax
from jax.experimental import pallas as pl
from jax.experimental.pallas import tpu as pltpu
from jax.sharding import Mesh
from jax.sharding import PartitionSpec as P

MESH = pl.DeviceIdType.MESH
NZ, NT = 8, 8
OFFSETS = (0, -1, 1, -2, 2, -3, 3, 4)
SLOT = {d % NZ: s for s, d in enumerate(OFFSETS)}
BF, F32 = jnp.bfloat16, jnp.float32
NT_DIMS = (((1,), (1,)), ((), ()))


def kernel(
    tokens, ids, probs, wg, wu, wd, sg, su, sd, out,
    gath, part, dd, xx, zin, zout, wgv, wuv, wdv, sgv, suv, sdv, idv, prv, hbuf, sbuf,
    tsb, tsi, fin, agi,
    loc_sem, snd_sem, ag_sem, dd_sem, xx_sem, zin_sem, ts_sem, ta_sem,
):
    z, xl, c = lax.axis_index("z"), lax.axis_index("xl"), lax.axis_index("c")
    y, xh = lax.axis_index("y"), lax.axis_index("xh")
    t = y * 2 + xh
    rows = tokens.shape[0]
    half = rows // 2
    width = wg.shape[0] // 2
    group = 4 * rows
    zup, zdn = {"z": lax.rem(z + 1, NZ)}, {"z": lax.rem(z + NZ - 1, NZ)}
    xup = {"xl": 1 - xl, "xh": lax.rem(xh + xl, 2)}
    xdn = {"xl": 1 - xl, "xh": lax.rem(xh + 1 - xl, 2)}
    mate = {"c": 1 - c}
    peers = []
    for i in range(1, NT):
        tp = lax.rem(t + i, NT)
        peers.append((tp, {"y": tp // 2, "xh": lax.rem(tp, 2)}))

    local = []

    def load(src, dst):
        cp = pltpu.make_async_copy(src, dst, loc_sem.at[len(local)])
        cp.start()
        local.append(cp)
        return cp

    own = xl * 2 + c
    tok_cp = load(tokens, gath.at[0, own])
    sh_cp = [load(sg, sgv), load(su, suv), load(sd, sdv)]
    rt_cp = [load(ids, idv), load(probs, prv), load(wg, wgv), load(wu, wuv), load(wd, wdv)]

    barrier = pltpu.get_barrier_semaphore()
    greeted = [zup, zdn, xup, xdn, mate] + [p for _, p in peers]
    for dev in greeted:
        pl.semaphore_signal(barrier, inc=1, device_id=dev, device_id_type=MESH)
    pl.semaphore_wait(barrier, len(greeted))

    sent = []

    def send(src, dst, sem, dev):
        cp = pltpu.make_async_remote_copy(
            src_ref=src, dst_ref=dst, send_sem=snd_sem.at[len(sent)], recv_sem=sem,
            device_id=dev, device_id_type=MESH,
        )
        cp.start()
        sent.append(cp)

    def arrive(dst, sem):
        pltpu.make_async_remote_copy(
            src_ref=dst, dst_ref=dst, send_sem=snd_sem.at[0], recv_sem=sem,
            device_id=mate, device_id_type=MESH,
        ).wait_recv()

    def unit(slot, b, h):
        return gath.at[slot, b, pl.ds(h * half, half)]

    def spread(slot, b, h, from_z=True):
        ref, sem = unit(slot, b, h), ag_sem.at[slot, b, h]
        if from_z:
            send(ref, ref, sem, xup if h == 0 else xdn)
        send(ref, ref, sem, mate)

    def hop(offset, h, up):
        nxt = SLOT[(offset - 1 if up else offset + 1) % NZ]
        send(unit(SLOT[offset % NZ], own, h), unit(nxt, own, h), ag_sem.at[nxt, own, h], zup if up else zdn)

    def slots(k):
        return (0,) if k == 0 else (7,) if k == 4 else (2 * k - 1, 2 * k)

    def gather_z(k):
        for h in (0, 1):
            for up in (True, False):
                if k == 4 and up != (h == 0):
                    continue
                offset = -k if up else k
                slot = SLOT[offset % NZ]
                arrive(unit(slot, own, h), ag_sem.at[slot, own, h])
                if k < 3 or (k == 3 and up == (h == 0)):
                    hop(offset, h, up)
                spread(slot, own, h)

    def gather_x(k):
        b = (1 - xl) * 2 + c
        for h in (0, 1):
            for slot in slots(k):
                arrive(unit(slot, b, h), ag_sem.at[slot, b, h])
                spread(slot, b, h, from_z=False)

    def gather_mate(k):
        for slot in slots(k):
            for a in (0, 1):
                b = a * 2 + 1 - c
                for h in (0, 1):
                    arrive(unit(slot, b, h), ag_sem.at[slot, b, h])

    def ffn(x, g_ref, u_ref, d_ref, scale, write):
        m = x.shape[0]
        g = lax.dot_general(x, g_ref[...], NT_DIMS, preferred_element_type=F32)
        u = lax.dot_general(x, u_ref[...], NT_DIMS, preferred_element_type=F32)
        h = g / (1.0 + jnp.exp(-g)) * u
        if scale is not None:
            h = h * scale
        hbuf[pl.ds(0, m), :] = h.astype(BF)

        @pl.loop(0, 4)
        def _(n):
            cols = pl.ds(pl.multiple_of(n * 512, 512), 512)
            write(cols, jnp.dot(hbuf[pl.ds(0, m), :], d_ref[:, cols], preferred_element_type=F32))

    def column(slot, expert):
        gz = lax.rem(z + OFFSETS[slot] + NZ, NZ)
        lanes = pl.ds(pl.multiple_of(gz * group, group), group)
        row = jnp.sum(jnp.where(idv[:, lanes] == expert, prv[:, lanes], 0.0), axis=0, keepdims=True)
        return jnp.broadcast_to(row, (128, group)).T[:, :1]

    def compute(k):
        ss = slots(k)
        s0, ns = ss[0], len(ss)
        m = ns * group
        first = (z * 4 + xl * 2 + c) * 2
        w0, w1 = (
            jnp.concatenate([column(s, first + j) for s in ss], axis=0) for j in (0, 1)
        )
        lane = lax.broadcasted_iota(jnp.int32, (m, 2 * width), 1)
        scale = jnp.where(lane < width, w0, w1)

        def write(cols, p):
            part[pl.ds(s0, ns), :, :, cols] = p.astype(BF).reshape(ns, 4, rows, 512)

        ffn(gath[pl.ds(s0, ns)].reshape(m, gath.shape[-1]), wgv, wuv, wdv, scale, write)

    def swap_mate(k):
        for slot in slots(k):
            for a in (1 - xl, xl):
                send(part.at[slot, a * 2 + 1 - c], dd.at[slot, a], dd_sem.at[slot, a], mate)

    def swap_x(k):
        a = 1 - xl
        b = a * 2 + c
        for slot in slots(k):
            arrive(dd.at[slot, a], dd_sem.at[slot, a])
            part[slot, b] = (part[slot, b].astype(F32) + dd[slot, a].astype(F32)).astype(BF)
            for h, dev in ((0, xup), (1, xdn)):
                r = pl.ds(h * half, half)
                send(part.at[slot, b, r], xx.at[slot, r], xx_sem.at[slot, h], dev)

    seen = set()

    def ring_term(slot, h):
        if slot not in seen:
            seen.add(slot)
            arrive(dd.at[slot, xl], dd_sem.at[slot, xl])
        r = pl.ds(h * half, half)
        arrive(xx.at[slot, r], xx_sem.at[slot, h])
        return part[slot, own, r].astype(F32) + dd[slot, xl, r].astype(F32) + xx[slot, r].astype(F32)

    quarter = half // 2

    def ring(s):
        terms = [ring_term(SLOT[(-s if up else s) % NZ], h) for h, up in ((0, True), (1, False))]
        for q in (0, 1):
            r = pl.ds(q * quarter, quarter)
            for h, up in ((0, True), (1, False)):
                acc = terms[h][q * quarter : (q + 1) * quarter]
                if s > 1:
                    arrive(zin.at[h, s - 2, r], zin_sem.at[h, s - 2, q])
                    acc = acc + zin[h, s - 2, r].astype(F32)
                zout[h, s - 1, r] = acc.astype(BF)
                send(zout.at[h, s - 1, r], zin.at[h, s - 1, r], zin_sem.at[h, s - 1, q], zup if up else zdn)

    tok_cp.wait()
    for h in (0, 1):
        hop(0, h, True)
        hop(0, h, False)
        spread(0, own, h)

    for cp in sh_cp:
        cp.wait()

    def write_shared(cols, p):
        sbuf[:, cols] = p

    ffn(gath[0, own], sgv, suv, sdv, None, write_shared)
    for cp in rt_cp:
        cp.wait()
    gather_x(0)
    gather_mate(0)
    gather_z(1)
    compute(0)
    gather_x(1)
    gather_z(2)
    gather_mate(1)
    compute(1)
    swap_mate(1)
    gather_x(2)
    gather_z(3)
    swap_x(1)
    gather_mate(2)
    compute(2)
    swap_mate(2)
    gather_x(3)
    gather_z(4)
    ring(1)
    swap_x(2)
    gather_x(4)
    gather_mate(3)
    compute(3)
    swap_mate(3)
    ring(2)
    swap_x(3)
    gather_mate(4)
    compute(4)
    swap_mate(4)
    ring(3)
    swap_x(4)
    swap_mate(0)
    ring(4)
    swap_x(0)
    ring(5)
    ring(6)
    ring(7)
    for h in (0, 1):
        r = pl.ds(h * half, half)
        acc = ring_term(0, h) + sbuf[r, :]
        for q in (0, 1):
            rq = pl.ds(q * quarter, quarter)
            arrive(zin.at[h, NZ - 2, rq], zin_sem.at[h, NZ - 2, q])
        acc = (acc + zin[h, NZ - 2].astype(F32)).astype(BF)
        for i in range(NT):
            tsb[i, r, :] = acc[:, i * 256 : (i + 1) * 256]
    for tp, dev in peers:
        send(tsb.at[tp], tsi.at[t], ts_sem.at[t], dev)
    acc = tsb[t].astype(F32)
    for tp, _ in peers:
        arrive(tsi.at[tp], ts_sem.at[tp])
        acc = acc + tsi[tp].astype(F32)
    fin[...] = acc.astype(BF)
    for tp, dev in peers:
        send(fin, agi.at[t], ta_sem.at[t], dev)
    agi[t] = fin[...]
    for tp, _ in peers:
        arrive(agi.at[tp], ta_sem.at[tp])
    for i in range(NT):
        out[:, i * 256 : (i + 1) * 256] = agi[i]
    for cp in sent:
        cp.wait_send()


def layer(tokens, ids, probs, wg, wu, wd, sg, su, sd):
    rows, dim = tokens.shape
    hid = sg.shape[0]
    any_spec = pl.BlockSpec(memory_space=pl.ANY)
    wide = pltpu.VMEM((hid, dim), BF)
    dma = pltpu.SemaphoreType.DMA
    return pl.pallas_call(
        kernel,
        out_shape=jax.ShapeDtypeStruct((rows, dim), BF),
        in_specs=[any_spec] * 9,
        out_specs=pl.BlockSpec(memory_space=pltpu.VMEM),
        scratch_shapes=[
            pltpu.VMEM((NZ, 4, rows, dim), BF),
            pltpu.VMEM((NZ, 4, rows, dim), BF),
            pltpu.VMEM((NZ, 2, rows, dim), BF),
            pltpu.VMEM((NZ, rows, dim), BF),
            pltpu.VMEM((2, NZ - 1, rows // 2, dim), BF),
            pltpu.VMEM((2, NZ - 1, rows // 2, dim), BF),
            wide, wide, wide, wide, wide, wide,
            pltpu.VMEM(ids.shape, jnp.int32),
            pltpu.VMEM(probs.shape, F32),
            pltpu.VMEM((8 * rows, hid), BF),
            pltpu.VMEM((rows, dim), F32),
            pltpu.VMEM((NT, rows, dim // NT), BF),
            pltpu.VMEM((NT, rows, dim // NT), BF),
            pltpu.VMEM((rows, dim // NT), BF),
            pltpu.VMEM((NT, rows, dim // NT), BF),
            dma((9,)), dma((160,)), dma((NZ, 4, 2)), dma((NZ, 2)), dma((NZ, 2)),
            dma((2, NZ - 1, 2)), dma((NT,)), dma((NT,)),
        ],
        compiler_params=pltpu.CompilerParams(
            collective_id=0, has_side_effects=True, vmem_limit_bytes=60 * 1024 * 1024
        ),
    )(tokens, ids, probs, wg, wu, wd, sg, su, sd)


def body(tokens, expert_ids, gate_probs, w_gate, w_up, w_down, shared_gate, shared_up, shared_down):
    dim = tokens.shape[1]
    stacked = lambda w: jnp.swapaxes(w, 1, 2).reshape(-1, dim)
    return layer(
        tokens, expert_ids.T, gate_probs.T, stacked(w_gate), stacked(w_up), w_down.reshape(-1, dim),
        shared_gate.T, shared_up.T, shared_down,
    )


def solution(mesh):
    torus = Mesh(mesh.devices.reshape(NZ, 2, 2, 4, 2), ("z", "xl", "c", "y", "xh"))
    e, t = ("z", "xl", "c"), ("y", "xh")
    return jax.shard_map(
        body,
        mesh=torus,
        in_specs=(
            P(e, None), P(), P(),
            P(e, None, t), P(e, None, t), P(e, t, None),
            P(None, t), P(None, t), P(t, None),
        ),
        out_specs=P(e, None),
        check_vma=False,
    )
```

time: 218 us -> 101 us (0.46)
  waiting for transfers between devices: 152 us -> 0 us
  Pallas kernels: 0 us -> 98 us
  matrix products: 22.9 us -> 0 us
  between operations: 13.2 us -> 0.01 us
  starting transfers between devices: 13 us -> 0 us
  blocking collectives: 12.8 us -> 0 us
  other arithmetic: 2.23 us -> 0 us
    pallas_call x0 -> x1, Pallas kernels: none -> 98 us  [layer(): pl.pallas_call(kernel, out_shape=jax.ShapeDtypeStruct((rows, dim), BF), i...]
    all_gather x1 -> x0, waiting for transfers between devices: 74.2 us -> none  [body(): lax.all_gather(tokens, 'expert', axis=0, tiled=True)]
    reduce_scatter x2 -> x0, waiting for transfers between devices: 47.9 us -> none  [scatter_axes(): nearer = lax.psum_scatter(x, axes[0], scatter_dimension=dim, tiled=True)]
    all_to_all x2 -> x0, waiting for transfers between devices: 28.9 us -> none  [the longest x1 28.9 us: sent_and_summed(): blocks = lax.all_to_all(cut_along(x, dim, size), axis, 0, 0, tiled=True)]
    dot_general x8 -> x0, matrix products: 22.9 us -> none  [the longest x1 8.18 us: body(): jnp.einsum('lcr,rd->lcd', picker, lax.all_gather(tokens, 'expert', axis=0...]
    all_to_all x2 -> x0, starting transfers between devices: 12.9 us -> none  [the longest x1 8.63 us: sent_and_summed(): blocks = lax.all_to_all(cut_along(x, dim, size), axis, 0, 0, tiled=True)]
    all_to_all x1 -> x0, blocking collectives: 12.8 us -> none  [sent_to_all(): return lax.all_to_all(copies, axis, split_axis=0, concat_axis=0, tiled=True)]
  transfers between devices with their start and end apart: 5 -> 0, of which waited for: 4 -> 0; matrix products, arithmetic and copies ran while one was open for 5% -> 0% of each run, Pallas kernels for 0% -> 0%
where the time goes in v1:
time: 101 us; the launch traced here: 99.7 us
  Pallas kernels  98 us (97%)
  local copies, waits for them, and re-layouts  1.67 us (2%)
    pallas_call x1, Pallas kernels, layer(): pl.pallas_call(kernel, out_shape=jax.ShapeDtypeStruct((rows, dim), BF), i...  98 us

profile of v1, /device:TPU:2, one launch (start us, length us, event | category | flops | bytes accessed | tf_op | source)
XLA Modules:
  0.0 99.7 jit_solution(8499212262129537156)
XLA Ops:
  0.0 98.0 %shard_map.91 = bf16[64,2048]{1,0:T(8,128)(2,1)} custom-call(bf16[64,2048]{1,0:T(8,128)(2,1)} %tokens.1, s32[6,2048]{1,0:T(8,128)} %bitcast.16, f32[6,2048]{1,0:T(8,128)} %bitcast.17, bf16[352,2048]{1,0:T(8,128)(2,1)} %bitcast.11, bf16[352,2048]{1,0:T(8,128)(2,1)} %bitcast.12, bf16[352,2048]{1,0:T(8,128)(2,1)} %bitcast.13, bf16[352,2048]{1,0:T(8,128)(2,1)} %bitcast.14, ...), custom_call_target="tpu_custom_call" | custom-call | tf_op jit(solution)/shard_map/pallas_call | solution.py:275
  98.0 1.7 %copy.11 = bf16[64,2048]{1,0:T(8,128)(2,1)} copy(bf16[64,2048]{1,0:T(8,128)(2,1)} %shard_map.91) | data formatting | bytes 524288

commit v2 on v1

v2 whole, which is shorter than its diff:
```python
import jax
import jax.numpy as jnp
from jax import lax
from jax.experimental import pallas as pl
from jax.experimental.pallas import tpu as pltpu
from jax.sharding import Mesh
from jax.sharding import PartitionSpec as P

MESH = pl.DeviceIdType.MESH
NZ, NY = 8, 4
OFFSETS = (0, -1, 1, -2, 2, -3, 3, 4)
SLOT = {d % NZ: s for s, d in enumerate(OFFSETS)}
BF, F32 = jnp.bfloat16, jnp.float32
GA, GR = 512, 512
NT_DIMS = (((1,), (1,)), ((), ()))


def kernel(
    tokens, ids, probs, wg, wu, wd, sg, su, sd, out,
    gath, part, dd, yy, xx, zin, zout, wguv, wdv, sguv, sdv, idv, prv, hbuf, sbuf,
    tsb, tsi, fin, agi,
    loc_sem, snd_sem, ag_sem, ya_sem, ma_sem, dd_sem, yr_sem, xx_sem, zin_sem, ts_sem, ta_sem,
):
    z, xl, c = lax.axis_index("z"), lax.axis_index("xl"), lax.axis_index("c")
    y, xh = lax.axis_index("y"), lax.axis_index("xh")
    rows, dim = tokens.shape
    half, quarter = rows // 2, rows // 4
    width = wg.shape[0] // 2
    group = 4 * rows
    sa, sr = GA // NY, GR // NY
    ca, cr = dim - GA, dim - GR
    aw, rw = ca + sa, cr + sr
    zup, zdn = {"z": lax.rem(z + 1, NZ)}, {"z": lax.rem(z + NZ - 1, NZ)}
    xup = {"xl": 1 - xl, "xh": lax.rem(xh + xl, 2)}
    xdn = {"xl": 1 - xl, "xh": lax.rem(xh + 1 - xl, 2)}
    mate = {"c": 1 - c}
    yat = [lax.rem(y + i, NY) for i in range(NY)]
    peers = [(yat[i], lax.rem(xh + j, 2), i, j) for i in range(NY) for j in (0, 1)][1:]

    local = []

    def load(src, dst):
        cp = pltpu.make_async_copy(src, dst, loc_sem.at[len(local)])
        cp.start()
        local.append(cp)
        return cp

    def load_turned(src, dst, common, size):
        cps = [load(src.at[:, pl.ds(0, common)], dst.at[:, pl.ds(0, common)])]
        for i in range(NY if size else 0):
            at = pl.multiple_of(common + yat[i] * size, 128)
            cps.append(load(src.at[:, pl.ds(at, size)], dst.at[:, pl.ds(common + i * size, size)]))
        return cps

    def load_pair(g, u, dst):
        hid = g.shape[0]
        tail = hid - 256
        cps = []
        for src, at, n, to in ((g, 0, 256, 0), (u, 0, 256, 256), (g, 256, tail, 512), (u, 256, tail, 640)):
            cps += load_turned(src.at[pl.ds(at, n)], dst.at[pl.ds(to, n)], ca, sa)
        return cps

    own, other = c * 2 + xl, c * 2 + 1 - xl
    mine, mates = pl.ds(c * 2, 2), pl.ds((1 - c) * 2, 2)
    tok_cp = load_turned(tokens, gath.at[0, own], ca, sa)
    sh_cp = load_pair(sg, su, sguv) + load_turned(sd, sdv, cr, sr)
    rt_cp = [load(ids, idv), load(probs, prv)] + load_pair(wg, wu, wguv) + load_turned(wd, wdv, cr, sr)

    barrier = pltpu.get_barrier_semaphore()
    greeted = [zup, zdn, xup, xdn, mate] + [{"y": yp, "xh": xp} for yp, xp, _, _ in peers]
    for dev in greeted:
        pl.semaphore_signal(barrier, inc=1, device_id=dev, device_id_type=MESH)
    pl.semaphore_wait(barrier, len(greeted))

    sent = []

    def send(src, dst, sem, dev):
        cp = pltpu.make_async_remote_copy(
            src_ref=src, dst_ref=dst, send_sem=snd_sem.at[len(sent)], recv_sem=sem,
            device_id=dev, device_id_type=MESH,
        )
        cp.start()
        sent.append(cp)

    def arrive(dst, sem):
        pltpu.make_async_remote_copy(
            src_ref=dst, dst_ref=dst, send_sem=snd_sem.at[0], recv_sem=sem,
            device_id=mate, device_id_type=MESH,
        ).wait_recv()

    def slots(k):
        return (0,) if k == 0 else (7,) if k == 4 else (2 * k - 1, 2 * k)

    def unit(slot, b, h):
        return gath.at[slot, b, pl.ds(h * half, half), pl.ds(0, aw)]

    def hop(offset, h, up):
        nxt = SLOT[(offset - 1 if up else offset + 1) % NZ]
        send(unit(SLOT[offset % NZ], own, h), unit(nxt, own, h), ag_sem.at[nxt, 0, h], zup if up else zdn)

    def across(slot, h):
        send(unit(slot, own, h), unit(slot, own, h), ag_sem.at[slot, 1, h], xup if h == 0 else xdn)

    def gather_z(k):
        for h in (0, 1):
            for up in (True, False):
                if k == 4 and up != (h == 0):
                    continue
                offset = -k if up else k
                slot = SLOT[offset % NZ]
                arrive(unit(slot, own, h), ag_sem.at[slot, 0, h])
                if k < 3 or (k == 3 and up == (h == 0)):
                    hop(offset, h, up)
                across(slot, h)

    def fresh(slot):
        return pl.ds(other, 1) if slot == 0 else mine

    def main(slot):
        return gath.at[slot, fresh(slot), :, pl.ds(0, aw)]

    def piece(slot, i):
        return gath.at[slot, fresh(slot), :, pl.ds(ca + i * sa, sa)]

    def rest(slot):
        return gath.at[slot, fresh(slot), :, pl.ds(aw, dim - aw)]

    def gather_x(k):
        for slot in slots(k):
            for h in (0, 1):
                arrive(unit(slot, other, h), ag_sem.at[slot, 1, h])
            for i in range(1, NY if GA else 1):
                send(piece(slot, 0), piece(slot, NY - i), ya_sem.at[slot, NY - i - 1], {"y": yat[i]})
            send(main(slot), main(slot), ma_sem.at[slot, 0], mate)

    def gather_y(k):
        for slot in slots(k) if GA else ():
            for i in range(1, NY):
                arrive(piece(slot, i), ya_sem.at[slot, i - 1])
            send(rest(slot), rest(slot), ma_sem.at[slot, 1], mate)

    def gather_mate(k):
        for slot in slots(k):
            if slot == 0:
                arrive(gath.at[0, (1 - c) * 2 + xl], ma_sem.at[NZ, 0])
            blocks = pl.ds((1 - c) * 2 + 1 - xl, 1) if slot == 0 else mates
            arrive(gath.at[slot, blocks, :, pl.ds(0, aw)], ma_sem.at[slot, 0])
            if GA:
                arrive(gath.at[slot, blocks, :, pl.ds(aw, dim - aw)], ma_sem.at[slot, 1])

    def ffn(x, gu_ref, d_ref, scale, write):
        m = x.shape[0]
        hid = d_ref.shape[0]
        gu = lax.dot_general(x, gu_ref[...], NT_DIMS, preferred_element_type=F32)
        for at, g, u in (
            (0, gu[:, 0:256], gu[:, 256:512]),
            (256, gu[:, 512 : hid + 256], gu[:, 640 : hid + 384]),
        ):
            h = g / (1.0 + jnp.exp(-g)) * u
            if scale is not None:
                h = h * scale(at, h.shape[1])
            hbuf[pl.ds(0, m), pl.ds(at, h.shape[1])] = h.astype(BF)

        @pl.loop(0, 4)
        def _(n):
            cols = pl.ds(pl.multiple_of(n * 512, 512), 512)
            write(cols, jnp.dot(hbuf[pl.ds(0, m), :], d_ref[:, cols], preferred_element_type=F32))

    def column(slot, expert):
        gz = lax.rem(z + OFFSETS[slot] + NZ, NZ)
        lanes = pl.ds(pl.multiple_of(gz * group, group), group)
        row = jnp.sum(jnp.where(idv[:, lanes] == expert, prv[:, lanes], 0.0), axis=0, keepdims=True)
        col = jnp.broadcast_to(row, (128, group)).T
        return [col[b * rows : (b + 1) * rows, :1] for b in (0, 2, 1, 3)]

    def compute(k):
        ss = slots(k)
        s0, ns = ss[0], len(ss)
        m = ns * group
        first = (z * 4 + xl * 2 + c) * 2
        w0, w1 = (
            jnp.concatenate([w for s in ss for w in column(s, first + j)], axis=0) for j in (0, 1)
        )

        def scale(at, n):
            lane = at + lax.broadcasted_iota(jnp.int32, (m, n), 1)
            return jnp.where(lane < width, w0, w1)

        def write(cols, p):
            part[pl.ds(s0, ns), :, :, cols] = p.astype(BF).reshape(ns, 4, rows, 512)

        ffn(gath[pl.ds(s0, ns)].reshape(m, dim), wguv, wdv, scale, write)
        if k == 0:
            part[0, own] = (part[0, own].astype(F32) + sbuf[...]).astype(BF)

    def swap_mate(k):
        for slot in slots(k):
            send(part.at[slot, mates], dd.at[slot], dd_sem.at[slot], mate)

    def swap_y(k):
        for slot in slots(k):
            arrive(dd.at[slot], dd_sem.at[slot])
            if GR:
                cols = pl.ds(rw, dim - rw)
                both = part[slot, mine, :, cols].astype(F32) + dd[slot, :, :, cols].astype(F32)
                part[slot, mine, :, cols] = both.astype(BF)
            for i in range(1, NY if GR else 1):
                send(
                    part.at[slot, mine, :, pl.ds(cr + i * sr, sr)], yy.at[slot, NY - i - 1],
                    yr_sem.at[slot, NY - i - 1], {"y": yat[i]},
                )

    def summed(slot, b, x, r):
        common = part[slot, b, r, 0:cr].astype(F32) + dd[slot, x, r, 0:cr].astype(F32)
        if not GR:
            return [common]
        own_slice = part[slot, b, r, cr:rw].astype(F32) + dd[slot, x, r, cr:rw].astype(F32)
        for i in range(NY - 1):
            own_slice = own_slice + yy[slot, i, x, r].astype(F32)
        return [common, own_slice]

    bounds = [(0, cr), (cr, rw)][: 2 if GR else 1]

    def swap_x(k):
        for slot in slots(k):
            for i in range(NY - 1 if GR else 0):
                arrive(yy.at[slot, i], yr_sem.at[slot, i])
            for h, dev in ((0, xup), (1, xdn)):
                r = pl.ds(h * half, half)
                for (lo, hi), v in zip(bounds, summed(slot, other, 1 - xl, r)):
                    part[slot, other, r, lo:hi] = v.astype(BF)
                send(
                    part.at[slot, other, r, pl.ds(0, rw)], xx.at[slot, r], xx_sem.at[slot, h], dev
                )

    def ring(s):
        for h, up in ((0, True), (1, False)):
            slot = SLOT[(-s if up else s) % NZ]
            r = pl.ds(h * half, half)
            arrive(xx.at[slot, r], xx_sem.at[slot, h])
        for q in (0, 1):
            r = pl.ds(q * quarter, quarter)
            for h, up in ((0, True), (1, False)):
                slot = SLOT[(-s if up else s) % NZ]
                full = pl.ds(h * half + q * quarter, quarter)
                if s > 1:
                    arrive(zin.at[h, s - 2, r], zin_sem.at[h, s - 2, q])
                for (lo, hi), v in zip(bounds, summed(slot, own, xl, full)):
                    v = v + xx[slot, full, lo:hi].astype(F32)
                    if s > 1:
                        v = v + zin[h, s - 2, r, lo:hi].astype(F32)
                    zout[h, s - 1, r, lo:hi] = v.astype(BF)
                send(zout.at[h, s - 1, r], zin.at[h, s - 1, r], zin_sem.at[h, s - 1, q], zup if up else zdn)

    for cp in tok_cp:
        cp.wait()
    for h in (0, 1):
        hop(0, h, True)
        hop(0, h, False)
        across(0, h)
    send(gath.at[0, own], gath.at[0, own], ma_sem.at[NZ, 0], mate)

    for cp in sh_cp:
        cp.wait()

    def write_shared(cols, p):
        sbuf[:, cols] = p

    ffn(gath[0, own], sguv, sdv, None, write_shared)
    for cp in rt_cp:
        cp.wait()
    gather_z(1)
    gather_x(0)
    gather_y(0)
    gather_z(2)
    gather_x(1)
    gather_mate(0)
    compute(0)
    gather_y(1)
    gather_z(3)
    gather_x(2)
    gather_mate(1)
    compute(1)
    swap_mate(1)
    gather_y(2)
    gather_z(4)
    gather_x(3)
    swap_y(1)
    gather_mate(2)
    compute(2)
    swap_mate(2)
    gather_y(3)
    gather_x(4)
    swap_x(1)
    swap_y(2)
    gather_mate(3)
    compute(3)
    swap_mate(3)
    gather_y(4)
    ring(1)
    swap_x(2)
    swap_y(3)
    gather_mate(4)
    compute(4)
    swap_mate(4)
    swap_mate(0)
    ring(2)
    swap_x(3)
    swap_y(4)
    swap_y(0)
    ring(3)
    swap_x(4)
    swap_x(0)
    ring(4)
    ring(5)
    ring(6)
    ring(7)
    cw = cr // NY
    for h in (0, 1):
        r = pl.ds(h * half, half)
        arrive(xx.at[0, r], xx_sem.at[0, h])
        for q in (0, 1):
            rq = pl.ds(q * quarter, quarter)
            arrive(zin.at[h, NZ - 2, rq], zin_sem.at[h, NZ - 2, q])
        for (lo, hi), v in zip(bounds, summed(0, own, xl, r)):
            v = (v + xx[0, r, lo:hi].astype(F32) + zin[h, NZ - 2, :, lo:hi].astype(F32)).astype(BF)
            if lo == 0:
                for i in range(NY):
                    tsb[i, h, :, 0:cw] = v[:, i * cw : (i + 1) * cw]
            else:
                tsb[y, h, :, cw : cw + sr] = v
    for yp, xp, i, j in peers:
        n = cw + sr if i == 0 else cw
        send(
            tsb.at[yp, xp, :, pl.ds(0, n)], tsi.at[(NY - i) % NY, j, :, pl.ds(0, n)],
            ts_sem.at[(NY - i) % NY, j], {"y": yp, "xh": xp},
        )
    acc = tsb[y, xh, :, 0:cw].astype(F32)
    for _, _, i, j in peers:
        n = cw + sr if i == 0 else cw
        arrive(tsi.at[i, j, :, pl.ds(0, n)], ts_sem.at[i, j])
        acc = acc + tsi[i, j, :, 0:cw].astype(F32)
    fin[:, 0:cw] = acc.astype(BF)
    if GR:
        fin[:, cw : cw + sr] = (
            tsb[y, xh, :, cw : cw + sr].astype(F32) + tsi[0, 1, :, cw : cw + sr].astype(F32)
        ).astype(BF)
    for yp, xp, i, j in peers:
        send(fin, agi.at[y, xh], ta_sem.at[(NY - i) % NY, j], {"y": yp, "xh": xp})
    agi[y, xh] = fin[...]
    for yp, xp, i, j in peers:
        arrive(agi.at[yp, xp], ta_sem.at[i, j])
    for i in range(NY):
        for j in (0, 1):
            r = pl.ds(j * half, half)
            out[r, i * cw : (i + 1) * cw] = agi[i, j, :, 0:cw]
            if GR:
                out[r, cr + i * sr : cr + (i + 1) * sr] = agi[i, j, :, cw : cw + sr]
    for cp in sent:
        cp.wait_send()


def layer(tokens, ids, probs, wg, wu, wd, sg, su, sd):
    rows, dim = tokens.shape
    hid = sg.shape[0]
    rw = dim - GR + GR // NY
    any_spec = pl.BlockSpec(memory_space=pl.ANY)
    pair, down = pltpu.VMEM((hid + 384, dim), BF), pltpu.VMEM((hid, dim), BF)
    dma = pltpu.SemaphoreType.DMA
    last = (NY, 2, rows // 2, dim // NY)
    return pl.pallas_call(
        kernel,
        out_shape=jax.ShapeDtypeStruct((rows, dim), BF),
        in_specs=[any_spec] * 9,
        out_specs=pl.BlockSpec(memory_space=pltpu.VMEM),
        scratch_shapes=[
            pltpu.VMEM((NZ, 4, rows, dim), BF),
            pltpu.VMEM((NZ, 4, rows, dim), BF),
            pltpu.VMEM((NZ, 2, rows, dim), BF),
            pltpu.VMEM((NZ, NY - 1, 2, rows, max(GR // NY, 128)), BF),
            pltpu.VMEM((NZ, rows, rw), BF),
            pltpu.VMEM((2, NZ - 1, rows // 2, rw), BF),
            pltpu.VMEM((2, NZ - 1, rows // 2, rw), BF),
            pair, down, pair, down,
            pltpu.VMEM(ids.shape, jnp.int32),
            pltpu.VMEM(probs.shape, F32),
            pltpu.VMEM((8 * rows, hid), BF),
            pltpu.VMEM((rows, dim), F32),
            pltpu.VMEM(last, BF),
            pltpu.VMEM(last, BF),
            pltpu.VMEM(last[2:], BF),
            pltpu.VMEM(last, BF),
            dma((64,)), dma((200,)), dma((NZ, 2, 2)), dma((NZ, NY - 1)), dma((NZ + 1, 2)),
            dma((NZ,)), dma((NZ, NY - 1)), dma((NZ, 2)), dma((2, NZ - 1, 2)), dma((NY, 2)), dma((NY, 2)),
        ],
        compiler_params=pltpu.CompilerParams(
            collective_id=0, has_side_effects=True, vmem_limit_bytes=62 * 1024 * 1024
        ),
    )(tokens, ids, probs, wg, wu, wd, sg, su, sd)


def body(tokens, expert_ids, gate_probs, w_gate, w_up, w_down, shared_gate, shared_up, shared_down):
    dim = tokens.shape[1]
    stacked = lambda w: jnp.swapaxes(w, 1, 2).reshape(-1, dim)
    return layer(
        tokens, expert_ids.T, gate_probs.T, stacked(w_gate), stacked(w_up), w_down.reshape(-1, dim),
        shared_gate.T, shared_up.T, shared_down,
    )


def solution(mesh):
    torus = Mesh(mesh.devices.reshape(NZ, 2, 2, 4, 2), ("z", "xl", "c", "y", "xh"))
    e, t = ("z", "xl", "c"), ("y", "xh")
    return jax.shard_map(
        body,
        mesh=torus,
        in_specs=(
            P(e, None), P(), P(),
            P(e, None, t), P(e, None, t), P(e, t, None),
            P(None, t), P(None, t), P(t, None),
        ),
        out_specs=P(e, None),
        check_vma=False,
    )
```

time: 101 us -> 96.7 us (0.957); the launches traced: 99.7 us -> 96.6 us
  Pallas kernels: 98 us -> 94.9 us
    pallas_call x1, Pallas kernels: 98 us -> 94.9 us  [layer(): pl.pallas_call(kernel, out_shape=jax.ShapeDtypeStruct((rows, dim), BF), i...]
where the time goes in v2:
time: 96.7 us; the launch traced here: 96.6 us
  Pallas kernels  94.9 us (98%)
  local copies, waits for them, and re-layouts  1.67 us (2%)
    pallas_call x1, Pallas kernels, layer(): pl.pallas_call(kernel, out_shape=jax.ShapeDtypeStruct((rows, dim), BF), i...  94.9 us

profile of v2, /device:TPU:2, one launch (start us, length us, event | category | flops | bytes accessed | tf_op | source)
XLA Modules:
  0.0 96.6 jit_solution(16486636957280256143)
XLA Ops:
  0.0 94.9 %shard_map.91 = bf16[64,2048]{1,0:T(8,128)(2,1)} custom-call(bf16[64,2048]{1,0:T(8,128)(2,1)} %tokens.1, s32[6,2048]{1,0:T(8,128)} %bitcast.16, f32[6,2048]{1,0:T(8,128)} %bitcast.17, bf16[352,2048]{1,0:T(8,128)(2,1)} %bitcast.11, bf16[352,2048]{1,0:T(8,128)(2,1)} %bitcast.12, bf16[352,2048]{1,0:T(8,128)(2,1)} %bitcast.13, bf16[352,2048]{1,0:T(8,128)(2,1)} %bitcast.14, ...), custom_call_target="tpu_custom_call" | custom-call | tf_op jit(solution)/shard_map/pallas_call | solution.py:371
  94.9 1.7 %copy.11 = bf16[64,2048]{1,0:T(8,128)(2,1)} copy(bf16[64,2048]{1,0:T(8,128)(2,1)} %shard_map.91) | data formatting | bytes 524288

commit v3 on v2

v3 whole, which is shorter than its diff:
```python
import jax
import jax.numpy as jnp
from jax import lax
from jax.experimental import pallas as pl
from jax.experimental.pallas import tpu as pltpu
from jax.sharding import Mesh
from jax.sharding import PartitionSpec as P

MESH = pl.DeviceIdType.MESH
NZ, NY = 8, 4
OFFSETS = (0, -1, 1, -2, 2, -3, 3, 4)
SLOT = {d % NZ: s for s, d in enumerate(OFFSETS)}
BF, F32 = jnp.bfloat16, jnp.float32
GA, GR = 512, 512
NT_DIMS = (((1,), (1,)), ((), ()))


def kernel(
    tokens, ids, probs, wg, wu, wd, sg, su, sd, out,
    gath, part, yy, xx, zin, zout, wguv, wdv, sguv, sdv, idv, prv, wsc, hbuf, sbuf,
    tsb, tsi, fin, agi,
    loc_sem, snd_sem, wt_sem, ag_sem, ya_sem, yr_sem, xx_sem, zin_sem, ts_sem, ta_sem,
):
    z, xl, c = lax.axis_index("z"), lax.axis_index("xl"), lax.axis_index("c")
    y, xh = lax.axis_index("y"), lax.axis_index("xh")
    rows, dim = tokens.shape
    half, quarter = rows // 2, rows // 4
    hid = wg.shape[0]
    width = hid // 2
    sa, sr = GA // NY, GR // NY
    ca, cr = dim - GA, dim - GR
    aw, rw = ca + sa, cr + sr
    zup, zdn = {"z": lax.rem(z + 1, NZ)}, {"z": lax.rem(z + NZ - 1, NZ)}
    xup = {"xl": 1 - xl, "xh": lax.rem(xh + xl, 2)}
    xdn = {"xl": 1 - xl, "xh": lax.rem(xh + 1 - xl, 2)}
    mate = {"c": 1 - c}
    yat = [lax.rem(y + i, NY) for i in range(NY)]
    peers = [(yat[i], lax.rem(xh + j, 2), i, j) for i in range(NY) for j in (0, 1)][1:]
    other = 1 - xl

    local = []

    def load(src, dst):
        cp = pltpu.make_async_copy(src, dst, loc_sem.at[len(local)])
        cp.start()
        local.append(cp)
        return cp

    def load_turned(src, dst, common, size):
        cps = [load(src.at[:, pl.ds(0, common)], dst.at[:, pl.ds(0, common)])]
        for i in range(NY if size else 0):
            at = pl.multiple_of(common + yat[i] * size, 128)
            cps.append(load(src.at[:, pl.ds(at, size)], dst.at[:, pl.ds(common + i * size, size)]))
        return cps

    def at_rows(ref, first):
        return ref.at[pl.ds(first, hid)]

    tok_cp = load_turned(tokens, gath.at[0, xl], ca, sa)
    rt_cp = (
        load_turned(wg, at_rows(wguv, 0), ca, sa)
        + load_turned(wu, at_rows(wguv, 2 * hid), ca, sa)
        + load_turned(wd, at_rows(wdv, 0), cr, sr)
    )
    id_cp = [load(ids, idv), load(probs, prv)]
    sh_cp = (
        load_turned(sg, at_rows(sguv, 0), ca, sa)
        + load_turned(su, at_rows(sguv, hid), ca, sa)
        + load_turned(sd, sdv, cr, sr)
    )

    barrier = pltpu.get_barrier_semaphore()
    greeted = [zup, zdn, xup, xdn, mate] + [{"y": yp, "xh": xp} for yp, xp, _, _ in peers]
    for dev in greeted:
        pl.semaphore_signal(barrier, inc=1, device_id=dev, device_id_type=MESH)
    with jax.named_scope("barrier"):
        pl.semaphore_wait(barrier, len(greeted))

    sent = []

    def send(src, dst, sem, dev):
        cp = pltpu.make_async_remote_copy(
            src_ref=src, dst_ref=dst, send_sem=snd_sem.at[len(sent)], recv_sem=sem,
            device_id=dev, device_id_type=MESH,
        )
        cp.start()
        sent.append(cp)

    def arrive(dst, sem):
        pltpu.make_async_remote_copy(
            src_ref=dst, dst_ref=dst, send_sem=snd_sem.at[0], recv_sem=sem,
            device_id=mate, device_id_type=MESH,
        ).wait_recv()

    def slots(k):
        return (0,) if k == 0 else (7,) if k == 4 else (2 * k - 1, 2 * k)

    def unit(slot, b, h):
        return gath.at[slot, b, pl.ds(h * half, half), pl.ds(0, aw)]

    def hop(offset, h, up):
        nxt = SLOT[(offset - 1 if up else offset + 1) % NZ]
        send(unit(SLOT[offset % NZ], xl, h), unit(nxt, xl, h), ag_sem.at[nxt, 0, h], zup if up else zdn)

    def across(slot, h):
        send(unit(slot, xl, h), unit(slot, xl, h), ag_sem.at[slot, 1, h], xup if h == 0 else xdn)

    def gather_z(k):
        for h in (0, 1):
            for up in (True, False):
                if k == 4 and up != (h == 0):
                    continue
                offset = -k if up else k
                slot = SLOT[offset % NZ]
                arrive(unit(slot, xl, h), ag_sem.at[slot, 0, h])
                if k < 3 or (k == 3 and up == (h == 0)):
                    hop(offset, h, up)
                across(slot, h)

    def piece(slot, i):
        blocks = pl.ds(other, 1) if slot == 0 else pl.ds(0, 2)
        return gath.at[slot, blocks, :, pl.ds(ca + i * sa, sa)]

    def gather_x(k):
        for slot in slots(k):
            for h in (0, 1):
                arrive(unit(slot, other, h), ag_sem.at[slot, 1, h])
            for i in range(1, NY if GA else 1):
                send(piece(slot, 0), piece(slot, NY - i), ya_sem.at[slot, NY - i - 1], {"y": yat[i]})

    def gather_y(k):
        for slot in slots(k) if GA else ():
            for i in range(1, NY):
                arrive(piece(slot, i), ya_sem.at[slot, i - 1])

    def ffn(x, gu_ref, d_ref, scales, write):
        m = x.shape[0]
        n = d_ref.shape[0]
        gu = lax.dot_general(gu_ref[...], x, NT_DIMS, preferred_element_type=F32)
        if scales is None:
            g, u = gu[:n], gu[n:]
            h = g / (1.0 + jnp.exp(-g)) * u
        else:
            hs = []
            for j, scale in enumerate(scales):
                g, u = gu[j * width : (j + 1) * width], gu[n + j * width : n + (j + 1) * width]
                hs.append(g / (1.0 + jnp.exp(-g)) * u * scale)
            h = jnp.concatenate(hs, axis=0)
        hbuf[pl.ds(0, m), pl.ds(0, n)] = h.T.astype(BF)

        @pl.loop(0, 4)
        def _(i):
            cols = pl.ds(pl.multiple_of(i * 512, 512), 512)
            write(cols, jnp.dot(hbuf[pl.ds(0, m), pl.ds(0, n)], d_ref[:, cols], preferred_element_type=F32))

    def weigh():
        group, pair = 4 * rows, 2 * rows
        lane = lax.broadcasted_iota(jnp.int32, (8, pair), 1)
        for slot, offset in enumerate(OFFSETS):
            gz = lax.rem(z + offset + NZ, NZ)
            lanes = pl.ds(pl.multiple_of(gz * group, group), group)
            for j in range(4):
                expert = (z * 4 + xl * 2 + (c if j < 2 else 1 - c)) * 2 + j % 2
                row = jnp.sum(jnp.where(idv[:, lanes] == expert, prv[:, lanes], 0.0), axis=0, keepdims=True)
                lo, hi = (jnp.broadcast_to(row[:, at : at + pair], (8, pair)) for at in (0, pair))
                even = jnp.where(lane < rows, lo, pltpu.roll(hi, rows, 1))
                odd = jnp.where(lane < rows, pltpu.roll(lo, rows, 1), hi)
                wsc[j : j + 1, slot * pair : (slot + 1) * pair] = jnp.where(c == 0, even, odd)[0:1]

    def compute(k):
        ss = slots(k)
        s0, ns = ss[0], len(ss)
        pair = 2 * rows
        scales = [wsc[j : j + 1, s0 * pair : (s0 + ns) * pair] for j in range(4)]

        def write(cols, p):
            part[pl.ds(s0, ns), :, :, cols] = p.astype(BF).reshape(ns, 2, rows, 512)

        ffn(gath[pl.ds(s0, ns)].reshape(ns * pair, dim), wguv, wdv, scales, write)
        if k == 0:
            part[0, xl] = (part[0, xl].astype(F32) + sbuf[...]).astype(BF)

    sides = ((0, xup), (1, xdn))

    def x_send(slot, h, dev, lo, n, which):
        r = pl.ds(h * half, half)
        cols = pl.ds(lo, n)
        send(part.at[slot, other, r, cols], xx.at[slot, r, cols], xx_sem.at[slot, h, which], dev)

    def swap_y(k):
        for slot in slots(k):
            for h, dev in sides:
                x_send(slot, h, dev, 0, cr, 0)
            for i in range(1, NY if GR else 1):
                send(
                    part.at[slot, :, :, pl.ds(cr + i * sr, sr)], yy.at[slot, NY - i - 1],
                    yr_sem.at[slot, NY - i - 1], {"y": yat[i]},
                )

    def sliced(slot, b, r):
        v = part[slot, b, r, cr:rw].astype(F32)
        for i in range(NY - 1):
            v = v + yy[slot, i, b, r].astype(F32)
        return v

    def summed(slot, r):
        common = part[slot, xl, r, 0:cr].astype(F32)
        return [common, sliced(slot, xl, r)] if GR else [common]

    bounds = [(0, cr), (cr, rw)][: 2 if GR else 1]

    def swap_x(k):
        for slot in slots(k) if GR else ():
            for i in range(NY - 1):
                arrive(yy.at[slot, i], yr_sem.at[slot, i])
            part[slot, other, :, cr:rw] = sliced(slot, other, slice(None)).astype(BF)
            for h, dev in sides:
                x_send(slot, h, dev, cr, sr, 1)

    def x_arrive(slot, h):
        r = pl.ds(h * half, half)
        for which, (lo, hi) in enumerate(bounds):
            arrive(xx.at[slot, r, pl.ds(lo, hi - lo)], xx_sem.at[slot, h, which])

    def ring(s):
        for h, up in ((0, True), (1, False)):
            x_arrive(SLOT[(-s if up else s) % NZ], h)
        for q in (0, 1):
            r = pl.ds(q * quarter, quarter)
            for h, up in ((0, True), (1, False)):
                slot = SLOT[(-s if up else s) % NZ]
                full = pl.ds(h * half + q * quarter, quarter)
                if s > 1:
                    arrive(zin.at[h, s - 2, r], zin_sem.at[h, s - 2, q])
                for (lo, hi), v in zip(bounds, summed(slot, full)):
                    v = v + xx[slot, full, lo:hi].astype(F32)
                    if s > 1:
                        v = v + zin[h, s - 2, r, lo:hi].astype(F32)
                    zout[h, s - 1, r, lo:hi] = v.astype(BF)
                send(zout.at[h, s - 1, r], zin.at[h, s - 1, r], zin_sem.at[h, s - 1, q], zup if up else zdn)

    for cp in tok_cp:
        cp.wait()
    for h in (0, 1):
        hop(0, h, True)
        hop(0, h, False)
        across(0, h)
    for cp in rt_cp:
        cp.wait()
    moved = ((wguv, 0), (wguv, 2 * hid), (wdv, 0))
    for i, (ref, at) in enumerate(moved):
        send(at_rows(ref, at), at_rows(ref, at + hid), wt_sem.at[i], mate)
    for cp in id_cp + sh_cp:
        cp.wait()

    def write_shared(cols, p):
        sbuf[:, cols] = p

    with jax.named_scope("shared"):
        ffn(gath[0, xl], sguv, sdv, None, write_shared)
    with jax.named_scope("weigh"):
        weigh()

    def weights():
        for i, (ref, at) in enumerate(moved):
            arrive(at_rows(ref, at + hid), wt_sem.at[i])

    with jax.named_scope("s00_gz1"):
        gather_z(1)
    with jax.named_scope("s01_gx0"):
        gather_x(0)
    with jax.named_scope("s02_gy0"):
        gather_y(0)
    with jax.named_scope("s03_w"):
        weights()
    with jax.named_scope("s04_c0"):
        compute(0)
    with jax.named_scope("s05_gz2"):
        gather_z(2)
    with jax.named_scope("s06_gx1"):
        gather_x(1)
    with jax.named_scope("s07_gy1"):
        gather_y(1)
    with jax.named_scope("s08_c1"):
        compute(1)
    with jax.named_scope("s09_sy1"):
        swap_y(1)
    with jax.named_scope("s10_gz3"):
        gather_z(3)
    with jax.named_scope("s11_gx2"):
        gather_x(2)
    with jax.named_scope("s12_sx1"):
        swap_x(1)
    with jax.named_scope("s13_gy2"):
        gather_y(2)
    with jax.named_scope("s14_c2"):
        compute(2)
    with jax.named_scope("s15_sy2"):
        swap_y(2)
    with jax.named_scope("s16_gz4"):
        gather_z(4)
    with jax.named_scope("s17_gx3"):
        gather_x(3)
    with jax.named_scope("s18_r1"):
        ring(1)
    with jax.named_scope("s19_sx2"):
        swap_x(2)
    with jax.named_scope("s20_gy3"):
        gather_y(3)
    with jax.named_scope("s21_c3"):
        compute(3)
    with jax.named_scope("s22_sy3"):
        swap_y(3)
    with jax.named_scope("s23_gx4"):
        gather_x(4)
    with jax.named_scope("s24_r2"):
        ring(2)
    with jax.named_scope("s25_sx3"):
        swap_x(3)
    with jax.named_scope("s26_gy4"):
        gather_y(4)
    with jax.named_scope("s27_c4"):
        compute(4)
    with jax.named_scope("s28_sy4"):
        swap_y(4)
    with jax.named_scope("s29_sy0"):
        swap_y(0)
    with jax.named_scope("s30_r3"):
        ring(3)
    with jax.named_scope("s31_sx4"):
        swap_x(4)
    with jax.named_scope("s32_sx0"):
        swap_x(0)
    with jax.named_scope("s33_r4"):
        ring(4)
    with jax.named_scope("s34_r5"):
        ring(5)
    with jax.named_scope("s35_r6"):
        ring(6)
    with jax.named_scope("s36_r7"):
        ring(7)
    cw = cr // NY
    with jax.named_scope("final"):
        for h in (0, 1):
            r = pl.ds(h * half, half)
            x_arrive(0, h)
            for q in (0, 1):
                rq = pl.ds(q * quarter, quarter)
                arrive(zin.at[h, NZ - 2, rq], zin_sem.at[h, NZ - 2, q])
            for (lo, hi), v in zip(bounds, summed(0, r)):
                v = (v + xx[0, r, lo:hi].astype(F32) + zin[h, NZ - 2, :, lo:hi].astype(F32)).astype(BF)
                if lo == 0:
                    for i in range(NY):
                        tsb[i, h, :, 0:cw] = v[:, i * cw : (i + 1) * cw]
                else:
                    tsb[y, h, :, cw : cw + sr] = v
    with jax.named_scope("tensor_sum"):
        for yp, xp, i, j in peers:
            n = cw + sr if i == 0 else cw
            send(
                tsb.at[yp, xp, :, pl.ds(0, n)], tsi.at[(NY - i) % NY, j, :, pl.ds(0, n)],
                ts_sem.at[(NY - i) % NY, j], {"y": yp, "xh": xp},
            )
        acc = tsb[y, xh, :, 0:cw].astype(F32)
        for _, _, i, j in peers:
            n = cw + sr if i == 0 else cw
            arrive(tsi.at[i, j, :, pl.ds(0, n)], ts_sem.at[i, j])
            acc = acc + tsi[i, j, :, 0:cw].astype(F32)
        fin[:, 0:cw] = acc.astype(BF)
        if GR:
            fin[:, cw : cw + sr] = (
                tsb[y, xh, :, cw : cw + sr].astype(F32) + tsi[0, 1, :, cw : cw + sr].astype(F32)
            ).astype(BF)
    with jax.named_scope("tensor_all"):
        for yp, xp, i, j in peers:
            send(fin, agi.at[y, xh], ta_sem.at[(NY - i) % NY, j], {"y": yp, "xh": xp})
        agi[y, xh] = fin[...]
        for yp, xp, i, j in peers:
            arrive(agi.at[yp, xp], ta_sem.at[i, j])
        for i in range(NY):
            for j in (0, 1):
                r = pl.ds(j * half, half)
                out[r, i * cw : (i + 1) * cw] = agi[i, j, :, 0:cw]
                if GR:
                    out[r, cr + i * sr : cr + (i + 1) * sr] = agi[i, j, :, cw : cw + sr]
    with jax.named_scope("sends"):
        for cp in sent:
            cp.wait_send()


def layer(tokens, ids, probs, wg, wu, wd, sg, su, sd):
    rows, dim = tokens.shape
    hid = sg.shape[0]
    rw = dim - GR + GR // NY
    any_spec = pl.BlockSpec(memory_space=pl.ANY)
    dma = pltpu.SemaphoreType.DMA
    last = (NY, 2, rows // 2, dim // NY)
    return pl.pallas_call(
        kernel,
        out_shape=jax.ShapeDtypeStruct((rows, dim), BF),
        in_specs=[any_spec] * 9,
        out_specs=pl.BlockSpec(memory_space=pltpu.VMEM),
        scratch_shapes=[
            pltpu.VMEM((NZ, 2, rows, dim), BF),
            pltpu.VMEM((NZ, 2, rows, dim), BF),
            pltpu.VMEM((NZ, NY - 1, 2, rows, max(GR // NY, 128)), BF),
            pltpu.VMEM((NZ, rows, rw), BF),
            pltpu.VMEM((2, NZ - 1, rows // 2, rw), BF),
            pltpu.VMEM((2, NZ - 1, rows // 2, rw), BF),
            pltpu.VMEM((4 * hid, dim), BF),
            pltpu.VMEM((2 * hid, dim), BF),
            pltpu.VMEM((2 * hid, dim), BF),
            pltpu.VMEM((hid, dim), BF),
            pltpu.VMEM(ids.shape, jnp.int32),
            pltpu.VMEM(probs.shape, F32),
            pltpu.VMEM((8, NZ * 2 * rows), F32),
            pltpu.VMEM((4 * rows, 2 * hid), BF),
            pltpu.VMEM((rows, dim), F32),
            pltpu.VMEM(last, BF),
            pltpu.VMEM(last, BF),
            pltpu.VMEM(last[2:], BF),
            pltpu.VMEM(last, BF),
            dma((64,)), dma((200,)), dma((3,)), dma((NZ, 2, 2)), dma((NZ, NY - 1)),
            dma((NZ, NY - 1)), dma((NZ, 2, 2)), dma((2, NZ - 1, 2)), dma((NY, 2)), dma((NY, 2)),
        ],
        compiler_params=pltpu.CompilerParams(
            collective_id=0, has_side_effects=True, vmem_limit_bytes=62 * 1024 * 1024
        ),
    )(tokens, ids, probs, wg, wu, wd, sg, su, sd)


def body(tokens, expert_ids, gate_probs, w_gate, w_up, w_down, shared_gate, shared_up, shared_down):
    dim = tokens.shape[1]
    stacked = lambda w: jnp.swapaxes(w, 1, 2).reshape(-1, dim)
    return layer(
        tokens, expert_ids.T, gate_probs.T, stacked(w_gate), stacked(w_up), w_down.reshape(-1, dim),
        shared_gate.T, shared_up.T, shared_down,
    )


def solution(mesh):
    torus = Mesh(mesh.devices.reshape(NZ, 2, 2, 4, 2), ("z", "xl", "c", "y", "xh"))
    e, t = ("z", "xl", "c"), ("y", "xh")
    return jax.shard_map(
        body,
        mesh=torus,
        in_specs=(
            P(e, None), P(), P(),
            P(e, None, t), P(e, None, t), P(e, t, None),
            P(None, t), P(None, t), P(t, None),
        ),
        out_specs=P(e, None),
        check_vma=False,
    )
```

time: 96.7 us -> 99.1 us (1.025)
  Pallas kernels: 94.9 us -> 96.9 us
    pallas_call x1, Pallas kernels: 94.9 us -> 96.9 us  [layer(): pl.pallas_call(kernel, out_shape=jax.ShapeDtypeStruct((rows, dim), BF), i...]
where the time goes in v3:
time: 99.1 us; the launch traced here: 98.6 us
  Pallas kernels  96.9 us (98%)
  local copies, waits for them, and re-layouts  1.67 us (2%)
    pallas_call x1, Pallas kernels, layer(): pl.pallas_call(kernel, out_shape=jax.ShapeDtypeStruct((rows, dim), BF), i...  96.9 us

profile of v3, /device:TPU:2, one launch (start us, length us, event | category | flops | bytes accessed | tf_op | source)
XLA Modules:
  0.0 98.6 jit_solution(4753369163163336248)
XLA Ops:
  0.0 96.9 %shard_map.91 = bf16[64,2048]{1,0:T(8,128)(2,1)} custom-call(bf16[64,2048]{1,0:T(8,128)(2,1)} %tokens.1, s32[6,2048]{1,0:T(8,128)} %bitcast.16, f32[6,2048]{1,0:T(8,128)} %bitcast.17, bf16[352,2048]{1,0:T(8,128)(2,1)} %bitcast.11, bf16[352,2048]{1,0:T(8,128)(2,1)} %bitcast.12, bf16[352,2048]{1,0:T(8,128)(2,1)} %bitcast.13, bf16[352,2048]{1,0:T(8,128)(2,1)} %bitcast.14, ...), custom_call_target="tpu_custom_call" | custom-call | tf_op jit(solution)/shard_map/pallas_call | solution.py:398
  96.9 1.7 %copy.11 = bf16[64,2048]{1,0:T(8,128)(2,1)} copy(bf16[64,2048]{1,0:T(8,128)(2,1)} %shard_map.91) | data formatting | bytes 524288

commit v4 on v3

--- a/solution.py
+++ b/solution.py
@@ -19,7 +19,7 @@
     tokens, ids, probs, wg, wu, wd, sg, su, sd, out,
     gath, part, yy, xx, zin, zout, wguv, wdv, sguv, sdv, idv, prv, wsc, hbuf, sbuf,
     tsb, tsi, fin, agi,
-    loc_sem, snd_sem, wt_sem, ag_sem, ya_sem, yr_sem, xx_sem, zin_sem, ts_sem, ta_sem,
+    loc_sem, snd_sem, wt_sem, ag_sem, ax_sem, ya_sem, yr_sem, xx_sem, zin_sem, ts_sem, ta_sem,
 ):
     z, xl, c = lax.axis_index("z"), lax.axis_index("xl"), lax.axis_index("c")
     y, xh = lax.axis_index("y"), lax.axis_index("xh")
@@ -40,33 +40,34 @@
 
     local = []
 
-    def load(src, dst):
-        cp = pltpu.make_async_copy(src, dst, loc_sem.at[len(local)])
-        cp.start()
-        local.append(cp)
-        return cp
-
-    def load_turned(src, dst, common, size):
-        cps = [load(src.at[:, pl.ds(0, common)], dst.at[:, pl.ds(0, common)])]
-        for i in range(NY if size else 0):
-            at = pl.multiple_of(common + yat[i] * size, 128)
-            cps.append(load(src.at[:, pl.ds(at, size)], dst.at[:, pl.ds(common + i * size, size)]))
-        return cps
+    def load(src, dst, common=None, size=0):
+        sem = loc_sem.at[len(local)]
+        if size:
+            pltpu.make_async_copy(src.at[:, pl.ds(0, common)], dst.at[:, pl.ds(0, common)], sem).start()
+            for i in range(NY):
+                at = pl.multiple_of(common + yat[i] * size, 128)
+                pltpu.make_async_copy(
+                    src.at[:, pl.ds(at, size)], dst.at[:, pl.ds(common + i * size, size)], sem
+                ).start()
+        else:
+            pltpu.make_async_copy(src, dst, sem).start()
+        local.append(pltpu.make_async_copy(src, dst, sem))
+        return local[-1:]
 
     def at_rows(ref, first):
         return ref.at[pl.ds(first, hid)]
 
-    tok_cp = load_turned(tokens, gath.at[0, xl], ca, sa)
+    tok_cp = load(tokens, gath.at[0, xl], ca, sa)
     rt_cp = (
-        load_turned(wg, at_rows(wguv, 0), ca, sa)
-        + load_turned(wu, at_rows(wguv, 2 * hid), ca, sa)
-        + load_turned(wd, at_rows(wdv, 0), cr, sr)
+        load(wg, at_rows(wguv, 0), ca, sa)
+        + load(wu, at_rows(wguv, 2 * hid), ca, sa)
+        + load(wd, at_rows(wdv, 0), cr, sr)
     )
-    id_cp = [load(ids, idv), load(probs, prv)]
+    id_cp = load(ids, idv) + load(probs, prv)
     sh_cp = (
-        load_turned(sg, at_rows(sguv, 0), ca, sa)
-        + load_turned(su, at_rows(sguv, hid), ca, sa)
-        + load_turned(sd, sdv, cr, sr)
+        load(sg, at_rows(sguv, 0), ca, sa)
+        + load(su, at_rows(sguv, hid), ca, sa)
+        + load(sd, sdv, cr, sr)
     )
 
     barrier = pltpu.get_barrier_semaphore()
@@ -76,15 +77,19 @@
     with jax.named_scope("barrier"):
         pl.semaphore_wait(barrier, len(greeted))
 
-    sent = []
-
-    def send(src, dst, sem, dev):
-        cp = pltpu.make_async_remote_copy(
-            src_ref=src, dst_ref=dst, send_sem=snd_sem.at[len(sent)], recv_sem=sem,
-            device_id=dev, device_id_type=MESH,
-        )
-        cp.start()
-        sent.append(cp)
+    kinds = {}
+
+    def send(kind, src, dst, sem, dev):
+        pltpu.make_async_remote_copy(
+            src_ref=src, dst_ref=dst, send_sem=snd_sem.at[kinds.setdefault(kind, len(kinds))],
+            recv_sem=sem, device_id=dev, device_id_type=MESH,
+        ).start()
+
+    def all_sent(kind, whole):
+        pltpu.make_async_remote_copy(
+            src_ref=whole, dst_ref=whole, send_sem=snd_sem.at[kinds[kind]], recv_sem=snd_sem.at[0],
+            device_id=mate, device_id_type=MESH,
+        ).wait_send()
 
     def arrive(dst, sem):
         pltpu.make_async_remote_copy(
@@ -100,10 +105,10 @@
 
     def hop(offset, h, up):
         nxt = SLOT[(offset - 1 if up else offset + 1) % NZ]
-        send(unit(SLOT[offset % NZ], xl, h), unit(nxt, xl, h), ag_sem.at[nxt, 0, h], zup if up else zdn)
+        send("z", unit(SLOT[offset % NZ], xl, h), unit(nxt, xl, h), ag_sem.at[nxt, h], zup if up else zdn)
 
     def across(slot, h):
-        send(unit(slot, xl, h), unit(slot, xl, h), ag_sem.at[slot, 1, h], xup if h == 0 else xdn)
+        send("x", unit(slot, xl, h), unit(slot, xl, h), ax_sem.at[slot], xup if h == 0 else xdn)
 
     def gather_z(k):
         for h in (0, 1):
@@ -112,26 +117,24 @@
                     continue
                 offset = -k if up else k
                 slot = SLOT[offset % NZ]
-                arrive(unit(slot, xl, h), ag_sem.at[slot, 0, h])
+                arrive(unit(slot, xl, h), ag_sem.at[slot, h])
                 if k < 3 or (k == 3 and up == (h == 0)):
                     hop(offset, h, up)
                 across(slot, h)
 
-    def piece(slot, i):
+    def piece(slot, i, n=1):
         blocks = pl.ds(other, 1) if slot == 0 else pl.ds(0, 2)
-        return gath.at[slot, blocks, :, pl.ds(ca + i * sa, sa)]
+        return gath.at[slot, blocks, :, pl.ds(ca + i * sa, n * sa)]
 
     def gather_x(k):
         for slot in slots(k):
-            for h in (0, 1):
-                arrive(unit(slot, other, h), ag_sem.at[slot, 1, h])
+            arrive(gath.at[slot, other, :, pl.ds(0, aw)], ax_sem.at[slot])
             for i in range(1, NY if GA else 1):
-                send(piece(slot, 0), piece(slot, NY - i), ya_sem.at[slot, NY - i - 1], {"y": yat[i]})
+                send("y" if slot else "y0", piece(slot, 0), piece(slot, NY - i), ya_sem.at[slot], {"y": yat[i]})
 
     def gather_y(k):
         for slot in slots(k) if GA else ():
-            for i in range(1, NY):
-                arrive(piece(slot, i), ya_sem.at[slot, i - 1])
+            arrive(piece(slot, 1, NY - 1), ya_sem.at[slot])
 
     def ffn(x, gu_ref, d_ref, scales, write):
         m = x.shape[0]
@@ -185,7 +188,7 @@
     def x_send(slot, h, dev, lo, n, which):
         r = pl.ds(h * half, half)
         cols = pl.ds(lo, n)
-        send(part.at[slot, other, r, cols], xx.at[slot, r, cols], xx_sem.at[slot, h, which], dev)
+        send(f"xx{which}", part.at[slot, other, r, cols], xx.at[slot, r, cols], xx_sem.at[slot, h], dev)
 
     def swap_y(k):
         for slot in slots(k):
@@ -193,8 +196,8 @@
                 x_send(slot, h, dev, 0, cr, 0)
             for i in range(1, NY if GR else 1):
                 send(
-                    part.at[slot, :, :, pl.ds(cr + i * sr, sr)], yy.at[slot, NY - i - 1],
-                    yr_sem.at[slot, NY - i - 1], {"y": yat[i]},
+                    "yy", part.at[slot, :, :, pl.ds(cr + i * sr, sr)], yy.at[slot, NY - i - 1],
+                    yr_sem.at[slot], {"y": yat[i]},
                 )
 
     def sliced(slot, b, r):
@@ -211,16 +214,14 @@
 
     def swap_x(k):
         for slot in slots(k) if GR else ():
-            for i in range(NY - 1):
-                arrive(yy.at[slot, i], yr_sem.at[slot, i])
+            arrive(yy.at[slot], yr_sem.at[slot])
             part[slot, other, :, cr:rw] = sliced(slot, other, slice(None)).astype(BF)
             for h, dev in sides:
                 x_send(slot, h, dev, cr, sr, 1)
 
     def x_arrive(slot, h):
         r = pl.ds(h * half, half)
-        for which, (lo, hi) in enumerate(bounds):
-            arrive(xx.at[slot, r, pl.ds(lo, hi - lo)], xx_sem.at[slot, h, which])
+        arrive(xx.at[slot, r], xx_sem.at[slot, h])
 
     def ring(s):
         for h, up in ((0, True), (1, False)):
@@ -237,7 +238,7 @@
                     if s > 1:
                         v = v + zin[h, s - 2, r, lo:hi].astype(F32)
                     zout[h, s - 1, r, lo:hi] = v.astype(BF)
-                send(zout.at[h, s - 1, r], zin.at[h, s - 1, r], zin_sem.at[h, s - 1, q], zup if up else zdn)
+                send("zz", zout.at[h, s - 1, r], zin.at[h, s - 1, r], zin_sem.at[h, s - 1, q], zup if up else zdn)
 
     for cp in tok_cp:
         cp.wait()
@@ -249,7 +250,7 @@
         cp.wait()
     moved = ((wguv, 0), (wguv, 2 * hid), (wdv, 0))
     for i, (ref, at) in enumerate(moved):
-        send(at_rows(ref, at), at_rows(ref, at + hid), wt_sem.at[i], mate)
+        send(f"w{i}", at_rows(ref, at), at_rows(ref, at + hid), wt_sem.at[i], mate)
     for cp in id_cp + sh_cp:
         cp.wait()
 
@@ -269,68 +270,68 @@
         gather_z(1)
     with jax.named_scope("s01_gx0"):
         gather_x(0)
-    with jax.named_scope("s02_gy0"):
+    with jax.named_scope("s02_gz2"):
+        gather_z(2)
+    with jax.named_scope("s03_gx1"):
+        gather_x(1)
+    with jax.named_scope("s04_gy0"):
         gather_y(0)
-    with jax.named_scope("s03_w"):
+    with jax.named_scope("s05_w"):
         weights()
-    with jax.named_scope("s04_c0"):
+    with jax.named_scope("s06_c0"):
         compute(0)
-    with jax.named_scope("s05_gz2"):
-        gather_z(2)
-    with jax.named_scope("s06_gx1"):
-        gather_x(1)
-    with jax.named_scope("s07_gy1"):
+    with jax.named_scope("s07_gz3"):
+        gather_z(3)
+    with jax.named_scope("s08_gx2"):
+        gather_x(2)
+    with jax.named_scope("s09_gy1"):
         gather_y(1)
-    with jax.named_scope("s08_c1"):
+    with jax.named_scope("s10_c1"):
         compute(1)
-    with jax.named_scope("s09_sy1"):
+    with jax.named_scope("s11_sy1"):
         swap_y(1)
-    with jax.named_scope("s10_gz3"):
-        gather_z(3)
-    with jax.named_scope("s11_gx2"):
-        gather_x(2)
-    with jax.named_scope("s12_sx1"):
+    with jax.named_scope("s12_gz4"):
+        gather_z(4)
+    with jax.named_scope("s13_gx3"):
+        gather_x(3)
+    with jax.named_scope("s14_gy2"):
+        gather_y(2)
+    with jax.named_scope("s15_c2"):
+        compute(2)
+    with jax.named_scope("s16_sy2"):
+        swap_y(2)
+    with jax.named_scope("s17_sx1"):
         swap_x(1)
-    with jax.named_scope("s13_gy2"):
-        gather_y(2)
-    with jax.named_scope("s14_c2"):
-        compute(2)
-    with jax.named_scope("s15_sy2"):
-        swap_y(2)
-    with jax.named_scope("s16_gz4"):
-        gather_z(4)
-    with jax.named_scope("s17_gx3"):
-        gather_x(3)
-    with jax.named_scope("s18_r1"):
+    with jax.named_scope("s18_gx4"):
+        gather_x(4)
+    with jax.named_scope("s19_gy3"):
+        gather_y(3)
+    with jax.named_scope("s20_c3"):
+        compute(3)
+    with jax.named_scope("s21_sy3"):
+        swap_y(3)
+    with jax.named_scope("s22_r1"):
         ring(1)
-    with jax.named_scope("s19_sx2"):
+    with jax.named_scope("s23_sx2"):
         swap_x(2)
-    with jax.named_scope("s20_gy3"):
-        gather_y(3)
-    with jax.named_scope("s21_c3"):
-        compute(3)
-    with jax.named_scope("s22_sy3"):
-        swap_y(3)
-    with jax.named_scope("s23_gx4"):
-        gather_x(4)
-    with jax.named_scope("s24_r2"):
+    with jax.named_scope("s24_gy4"):
+        gather_y(4)
+    with jax.named_scope("s25_c4"):
+        compute(4)
+    with jax.named_scope("s26_sy4"):
+        swap_y(4)
+    with jax.named_scope("s27_sy0"):
+        swap_y(0)
+    with jax.named_scope("s28_sx3"):
+        swap_x(3)
+    with jax.named_scope("s29_r2"):
         ring(2)
-    with jax.named_scope("s25_sx3"):
-        swap_x(3)
-    with jax.named_scope("s26_gy4"):
-        gather_y(4)
-    with jax.named_scope("s27_c4"):
-        compute(4)
-    with jax.named_scope("s28_sy4"):
-        swap_y(4)
-    with jax.named_scope("s29_sy0"):
-        swap_y(0)
-    with jax.named_scope("s30_r3"):
+    with jax.named_scope("s30_sx4"):
+        swap_x(4)
+    with jax.named_scope("s31_sx0"):
+        swap_x(0)
+    with jax.named_scope("s32_r3"):
         ring(3)
-    with jax.named_scope("s31_sx4"):
-        swap_x(4)
-    with jax.named_scope("s32_sx0"):
-        swap_x(0)
     with jax.named_scope("s33_r4"):
         ring(4)
     with jax.named_scope("s34_r5"):
@@ -351,41 +352,56 @@
                 v = (v + xx[0, r, lo:hi].astype(F32) + zin[h, NZ - 2, :, lo:hi].astype(F32)).astype(BF)
                 if lo == 0:
                     for i in range(NY):
-                        tsb[i, h, :, 0:cw] = v[:, i * cw : (i + 1) * cw]
+                        tsb[2 * i + h, :, 0:cw] = v[:, i * cw : (i + 1) * cw]
                 else:
-                    tsb[y, h, :, cw : cw + sr] = v
+                    tsb[2 * y + h, :, cw : cw + sr] = v
+    me = 2 * y + xh
     with jax.named_scope("tensor_sum"):
         for yp, xp, i, j in peers:
             n = cw + sr if i == 0 else cw
             send(
-                tsb.at[yp, xp, :, pl.ds(0, n)], tsi.at[(NY - i) % NY, j, :, pl.ds(0, n)],
-                ts_sem.at[(NY - i) % NY, j], {"y": yp, "xh": xp},
+                "t0" if i == 0 else "t1", tsb.at[2 * yp + xp, :, pl.ds(0, n)],
+                tsi.at[2 * ((NY - i) % NY) + j, :, pl.ds(0, n)],
+                ts_sem.at[min(i, 1)], {"y": yp, "xh": xp},
             )
-        acc = tsb[y, xh, :, 0:cw].astype(F32)
-        for _, _, i, j in peers:
-            n = cw + sr if i == 0 else cw
-            arrive(tsi.at[i, j, :, pl.ds(0, n)], ts_sem.at[i, j])
-            acc = acc + tsi[i, j, :, 0:cw].astype(F32)
-        fin[:, 0:cw] = acc.astype(BF)
+        mate_sum, far_sums = tsi.at[1, :, pl.ds(0, cw + sr)], tsi.at[pl.ds(2, 6), :, pl.ds(0, cw)]
+        arrive(mate_sum, ts_sem.at[0])
+        acc = tsb[me, :, 0:cw].astype(F32) + tsi[1, :, 0:cw].astype(F32)
         if GR:
             fin[:, cw : cw + sr] = (
-                tsb[y, xh, :, cw : cw + sr].astype(F32) + tsi[0, 1, :, cw : cw + sr].astype(F32)
+                tsb[me, :, cw : cw + sr].astype(F32) + tsi[1, :, cw : cw + sr].astype(F32)
             ).astype(BF)
+        arrive(far_sums, ts_sem.at[1])
+        for i in range(2, 8):
+            acc = acc + tsi[i, :, 0:cw].astype(F32)
+        fin[:, 0:cw] = acc.astype(BF)
     with jax.named_scope("tensor_all"):
         for yp, xp, i, j in peers:
-            send(fin, agi.at[y, xh], ta_sem.at[(NY - i) % NY, j], {"y": yp, "xh": xp})
-        agi[y, xh] = fin[...]
-        for yp, xp, i, j in peers:
-            arrive(agi.at[yp, xp], ta_sem.at[i, j])
+            send("t2", fin, agi.at[me], ta_sem.at[0], {"y": yp, "xh": xp})
+        agi[me] = fin[...]
+        others = agi.at[pl.ds(0, 7)]
+        arrive(others, ta_sem.at[0])
         for i in range(NY):
             for j in (0, 1):
                 r = pl.ds(j * half, half)
-                out[r, i * cw : (i + 1) * cw] = agi[i, j, :, 0:cw]
+                out[r, i * cw : (i + 1) * cw] = agi[2 * i + j, :, 0:cw]
                 if GR:
-                    out[r, cr + i * sr : cr + (i + 1) * sr] = agi[i, j, :, cw : cw + sr]
-    with jax.named_scope("sends"):
-        for cp in sent:
-            cp.wait_send()
+                    out[r, cr + i * sr : cr + (i + 1) * sr] = agi[2 * i + j, :, cw : cw + sr]
+    all_sent("z", gath.at[pl.ds(0, 7), 0, :, pl.ds(0, aw)])
+    all_sent("x", gath.at[:, 0, :, pl.ds(0, aw)])
+    if GA:
+        all_sent("y", gath.at[pl.ds(0, 7), :, :, pl.ds(0, 3 * sa)])
+        all_sent("y0", gath.at[0, 0, :, pl.ds(0, 3 * sa)])
+    all_sent("xx0", part.at[:, 0, :, pl.ds(0, cr)])
+    if GR:
+        all_sent("xx1", part.at[:, 0, :, pl.ds(0, sr)])
+        all_sent("yy", yy)
+    all_sent("zz", zout)
+    for i, (ref, at) in enumerate(moved):
+        all_sent(f"w{i}", at_rows(ref, at))
+    all_sent("t0", mate_sum)
+    all_sent("t1", far_sums)
+    all_sent("t2", others)
 
 
 def layer(tokens, ids, probs, wg, wu, wd, sg, su, sd):
@@ -394,7 +410,7 @@
     rw = dim - GR + GR // NY
     any_spec = pl.BlockSpec(memory_space=pl.ANY)
     dma = pltpu.SemaphoreType.DMA
-    last = (NY, 2, rows // 2, dim // NY)
+    last = (2 * NY, rows // 2, dim // NY)
     return pl.pallas_call(
         kernel,
         out_shape=jax.ShapeDtypeStruct((rows, dim), BF),
@@ -418,10 +434,10 @@
             pltpu.VMEM((rows, dim), F32),
             pltpu.VMEM(last, BF),
             pltpu.VMEM(last, BF),
-            pltpu.VMEM(last[2:], BF),
+            pltpu.VMEM(last[1:], BF),
             pltpu.VMEM(last, BF),
-            dma((64,)), dma((200,)), dma((3,)), dma((NZ, 2, 2)), dma((NZ, NY - 1)),
-            dma((NZ, NY - 1)), dma((NZ, 2, 2)), dma((2, NZ - 1, 2)), dma((NY, 2)), dma((NY, 2)),
+            dma((9,)), dma((14,)), dma((3,)), dma((NZ, 2)), dma((NZ,)), dma((NZ,)),
+            dma((NZ,)), dma((NZ, 2)), dma((2, NZ - 1, 2)), dma((2,)), dma((1,)),
         ],
         compiler_params=pltpu.CompilerParams(
             collective_id=0, has_side_effects=True, vmem_limit_bytes=62 * 1024 * 1024

time: 99.1 us -> 87 us (0.88)
  Pallas kernels: 96.9 us -> 84.2 us
    pallas_call x1, Pallas kernels: 96.9 us -> 84.2 us  [layer(): pl.pallas_call(kernel, out_shape=jax.ShapeDtypeStruct((rows, dim), BF), i...]
where the time goes in v4:
time: 87 us; the launch traced here: 85.8 us
  Pallas kernels  84.2 us (97%)
  local copies, waits for them, and re-layouts  1.67 us (2%)
    pallas_call x1, Pallas kernels, layer(): pl.pallas_call(kernel, out_shape=jax.ShapeDtypeStruct((rows, dim), BF), i...  84.2 us

profile of v4, /device:TPU:2, one launch (start us, length us, event | category | flops | bytes accessed | tf_op | source)
XLA Modules:
  0.0 85.8 jit_solution(17848214553340436755)
XLA Ops:
  0.0 84.2 %shard_map.91 = bf16[64,2048]{1,0:T(8,128)(2,1)} custom-call(bf16[64,2048]{1,0:T(8,128)(2,1)} %tokens.1, s32[6,2048]{1,0:T(8,128)} %bitcast.16, f32[6,2048]{1,0:T(8,128)} %bitcast.17, bf16[352,2048]{1,0:T(8,128)(2,1)} %bitcast.11, bf16[352,2048]{1,0:T(8,128)(2,1)} %bitcast.12, bf16[352,2048]{1,0:T(8,128)(2,1)} %bitcast.13, bf16[352,2048]{1,0:T(8,128)(2,1)} %bitcast.14, ...), custom_call_target="tpu_custom_call" | custom-call | tf_op jit(solution)/shard_map/pallas_call | solution.py:414
  84.2 1.7 %copy.11 = bf16[64,2048]{1,0:T(8,128)(2,1)} copy(bf16[64,2048]{1,0:T(8,128)(2,1)} %shard_map.91) | data formatting | bytes 524288

commit v5 on v4

--- a/solution.py
+++ b/solution.py
@@ -12,6 +12,7 @@
 SLOT = {d % NZ: s for s, d in enumerate(OFFSETS)}
 BF, F32 = jnp.bfloat16, jnp.float32
 GA, GR = 512, 512
+DC = 512
 NT_DIMS = (((1,), (1,)), ((), ()))
 
 
@@ -60,7 +61,7 @@
     tok_cp = load(tokens, gath.at[0, xl], ca, sa)
     rt_cp = (
         load(wg, at_rows(wguv, 0), ca, sa)
-        + load(wu, at_rows(wguv, 2 * hid), ca, sa)
+        + load(wu, at_rows(wguv, hid), ca, sa)
         + load(wd, at_rows(wdv, 0), cr, sr)
     )
     id_cp = load(ids, idv) + load(probs, prv)
@@ -71,7 +72,7 @@
     )
 
     barrier = pltpu.get_barrier_semaphore()
-    greeted = [zup, zdn, xup, xdn, mate] + [{"y": yp, "xh": xp} for yp, xp, _, _ in peers]
+    greeted = [zup, zdn, xup, xdn, mate] + [{"y": yp} for yp in yat[1:]]
     for dev in greeted:
         pl.semaphore_signal(barrier, inc=1, device_id=dev, device_id_type=MESH)
     with jax.named_scope("barrier"):
@@ -139,21 +140,18 @@
     def ffn(x, gu_ref, d_ref, scales, write):
         m = x.shape[0]
         n = d_ref.shape[0]
-        gu = lax.dot_general(gu_ref[...], x, NT_DIMS, preferred_element_type=F32)
-        if scales is None:
-            g, u = gu[:n], gu[n:]
-            h = g / (1.0 + jnp.exp(-g)) * u
-        else:
-            hs = []
-            for j, scale in enumerate(scales):
-                g, u = gu[j * width : (j + 1) * width], gu[n + j * width : n + (j + 1) * width]
-                hs.append(g / (1.0 + jnp.exp(-g)) * u * scale)
-            h = jnp.concatenate(hs, axis=0)
-        hbuf[pl.ds(0, m), pl.ds(0, n)] = h.T.astype(BF)
-
-        @pl.loop(0, 4)
-        def _(i):
-            cols = pl.ds(pl.multiple_of(i * 512, 512), 512)
+        hs = []
+        for first in range(0, n, hid):
+            gu = lax.dot_general(
+                gu_ref[2 * first : 2 * (first + hid)], x, NT_DIMS, preferred_element_type=F32
+            )
+            for at in range(0, hid, width):
+                g, u = gu[at : at + width], gu[hid + at : hid + at + width]
+                h = g / (1.0 + jnp.exp(-g)) * u
+                hs.append(h if scales is None else h * scales[len(hs)])
+        hbuf[pl.ds(0, m), pl.ds(0, n)] = jnp.concatenate(hs, axis=0).T.astype(BF)
+        for lo in range(0, dim, DC):
+            cols = pl.ds(lo, DC)
             write(cols, jnp.dot(hbuf[pl.ds(0, m), pl.ds(0, n)], d_ref[:, cols], preferred_element_type=F32))
 
     def weigh():
@@ -177,7 +175,7 @@
         scales = [wsc[j : j + 1, s0 * pair : (s0 + ns) * pair] for j in range(4)]
 
         def write(cols, p):
-            part[pl.ds(s0, ns), :, :, cols] = p.astype(BF).reshape(ns, 2, rows, 512)
+            part[pl.ds(s0, ns), :, :, cols] = p.astype(BF).reshape(ns, 2, rows, DC)
 
         ffn(gath[pl.ds(s0, ns)].reshape(ns * pair, dim), wguv, wdv, scales, write)
         if k == 0:
@@ -185,20 +183,25 @@
 
     sides = ((0, xup), (1, xdn))
 
-    def x_send(slot, h, dev, lo, n, which):
-        r = pl.ds(h * half, half)
-        cols = pl.ds(lo, n)
-        send(f"xx{which}", part.at[slot, other, r, cols], xx.at[slot, r, cols], xx_sem.at[slot, h], dev)
+    def x_send(slot, h, dev, which):
+        r, cols = pl.ds(h * half, half), bounds[which]
+        send(
+            f"xx{which}", part.at[slot, other, r, cols], xx.at[slot, r, cols],
+            xx_sem.at[slot, h, which], dev,
+        )
+
+    bounds = (pl.ds(0, cr), pl.ds(cr, sr))
 
     def swap_y(k):
         for slot in slots(k):
-            for h, dev in sides:
-                x_send(slot, h, dev, 0, cr, 0)
-            for i in range(1, NY if GR else 1):
+            for i in range(1, NY):
                 send(
                     "yy", part.at[slot, :, :, pl.ds(cr + i * sr, sr)], yy.at[slot, NY - i - 1],
                     yr_sem.at[slot], {"y": yat[i]},
                 )
+        for slot in slots(k):
+            for h, dev in sides:
+                x_send(slot, h, dev, 0)
 
     def sliced(slot, b, r):
         v = part[slot, b, r, cr:rw].astype(F32)
@@ -206,39 +209,65 @@
             v = v + yy[slot, i, b, r].astype(F32)
         return v
 
-    def summed(slot, r):
-        common = part[slot, xl, r, 0:cr].astype(F32)
-        return [common, sliced(slot, xl, r)] if GR else [common]
-
-    bounds = [(0, cr), (cr, rw)][: 2 if GR else 1]
-
     def swap_x(k):
-        for slot in slots(k) if GR else ():
+        for slot in slots(k):
             arrive(yy.at[slot], yr_sem.at[slot])
             part[slot, other, :, cr:rw] = sliced(slot, other, slice(None)).astype(BF)
             for h, dev in sides:
-                x_send(slot, h, dev, cr, sr, 1)
-
-    def x_arrive(slot, h):
-        r = pl.ds(h * half, half)
-        arrive(xx.at[slot, r], xx_sem.at[slot, h])
+                x_send(slot, h, dev, 1)
+
+    def ring_step(s, which, r_in, r_full, sem, h, up):
+        slot = SLOT[(-s if up else s) % NZ]
+        cols = bounds[which]
+        v = xx[slot, r_full, cols].astype(F32)
+        v = v + (sliced(slot, xl, r_full) if which else part[slot, xl, r_full, cols].astype(F32))
+        if s > 1:
+            arrive(zin.at[h, s - 2, r_in, cols], sem(s - 2))
+            v = v + zin[h, s - 2, r_in, cols].astype(F32)
+        if s == NZ:
+            return v.astype(BF)
+        zout[h, s - 1, r_in, cols] = v.astype(BF)
+        send(
+            f"zz{which}", zout.at[h, s - 1, r_in, cols], zin.at[h, s - 1, r_in, cols],
+            sem(s - 1), zup if up else zdn,
+        )
+
+    directions = ((0, True), (1, False))
 
     def ring(s):
-        for h, up in ((0, True), (1, False)):
-            x_arrive(SLOT[(-s if up else s) % NZ], h)
+        for h, up in directions:
+            slot = SLOT[(-s if up else s) % NZ]
+            x_at = xx.at[slot, pl.ds(h * half, half), bounds[0]]
+            arrive(x_at, xx_sem.at[slot, h, 0])
         for q in (0, 1):
-            r = pl.ds(q * quarter, quarter)
-            for h, up in ((0, True), (1, False)):
-                slot = SLOT[(-s if up else s) % NZ]
-                full = pl.ds(h * half + q * quarter, quarter)
-                if s > 1:
-                    arrive(zin.at[h, s - 2, r], zin_sem.at[h, s - 2, q])
-                for (lo, hi), v in zip(bounds, summed(slot, full)):
-                    v = v + xx[slot, full, lo:hi].astype(F32)
-                    if s > 1:
-                        v = v + zin[h, s - 2, r, lo:hi].astype(F32)
-                    zout[h, s - 1, r, lo:hi] = v.astype(BF)
-                send("zz", zout.at[h, s - 1, r], zin.at[h, s - 1, r], zin_sem.at[h, s - 1, q], zup if up else zdn)
+            for h, up in directions:
+                v = ring_step(
+                    s, 0, pl.ds(q * quarter, quarter), pl.ds(h * half + q * quarter, quarter),
+                    lambda i: zin_sem.at[h, i, q], h, up,
+                )
+                for i in range(NY if s == NZ else 0):
+                    tsb[2 * i + h, q * quarter : (q + 1) * quarter, 0:cw] = v[:, i * cw : (i + 1) * cw]
+
+    def ring_slice(s):
+        for h, up in directions:
+            slot = SLOT[(-s if up else s) % NZ]
+            full = pl.ds(h * half, half)
+            arrive(xx.at[slot, full, bounds[1]], xx_sem.at[slot, h, 1])
+            v = ring_step(s, 1, pl.ds(0, half), full, lambda i: zin_sem.at[h, i, 2], h, up)
+            if s == NZ:
+                tsb[2 * y + h, :, cw : cw + sr] = v
+
+    cw = cr // NY
+
+    def tensor_send(far):
+        n = cw if far else cw + sr
+        for yp, xp, i, j in peers:
+            if far == min(i, 1):
+                send(
+                    f"t{far}", tsb.at[2 * yp + xp, :, pl.ds(0, n)],
+                    tsi.at[2 * ((NY - i) % NY) + j, :, pl.ds(0, n)],
+                    ts_sem.at[far], {"y": yp, "xh": xp},
+                )
 
     for cp in tok_cp:
         cp.wait()
@@ -248,9 +277,9 @@
         across(0, h)
     for cp in rt_cp:
         cp.wait()
-    moved = ((wguv, 0), (wguv, 2 * hid), (wdv, 0))
-    for i, (ref, at) in enumerate(moved):
-        send(f"w{i}", at_rows(ref, at), at_rows(ref, at + hid), wt_sem.at[i], mate)
+    moved = ((wguv, 2 * hid), (wdv, hid))
+    for i, (ref, n) in enumerate(moved):
+        send(f"w{i}", ref.at[pl.ds(0, n)], ref.at[pl.ds(n, n)], wt_sem.at[i], mate)
     for cp in id_cp + sh_cp:
         cp.wait()
 
@@ -263,8 +292,8 @@
         weigh()
 
     def weights():
-        for i, (ref, at) in enumerate(moved):
-            arrive(at_rows(ref, at + hid), wt_sem.at[i])
+        for i, (ref, n) in enumerate(moved):
+            arrive(ref.at[pl.ds(n, n)], wt_sem.at[i])
 
     with jax.named_scope("s00_gz1"):
         gather_z(1)
@@ -288,10 +317,10 @@
         gather_y(1)
     with jax.named_scope("s10_c1"):
         compute(1)
-    with jax.named_scope("s11_sy1"):
+    with jax.named_scope("s11_gz4"):
+        gather_z(4)
+    with jax.named_scope("s12_sy1"):
         swap_y(1)
-    with jax.named_scope("s12_gz4"):
-        gather_z(4)
     with jax.named_scope("s13_gx3"):
         gather_x(3)
     with jax.named_scope("s14_gy2"):
@@ -306,71 +335,69 @@
         gather_x(4)
     with jax.named_scope("s19_gy3"):
         gather_y(3)
-    with jax.named_scope("s20_c3"):
+    with jax.named_scope("s20_r1"):
+        ring(1)
+    with jax.named_scope("s21_c3"):
         compute(3)
-    with jax.named_scope("s21_sy3"):
+    with jax.named_scope("s22_sy3"):
         swap_y(3)
-    with jax.named_scope("s22_r1"):
-        ring(1)
     with jax.named_scope("s23_sx2"):
         swap_x(2)
     with jax.named_scope("s24_gy4"):
         gather_y(4)
-    with jax.named_scope("s25_c4"):
+    with jax.named_scope("s25_r2"):
+        ring(2)
+    with jax.named_scope("s26_q1"):
+        ring_slice(1)
+    with jax.named_scope("s27_c4"):
         compute(4)
-    with jax.named_scope("s26_sy4"):
+    with jax.named_scope("s28_sy4"):
         swap_y(4)
-    with jax.named_scope("s27_sy0"):
+    with jax.named_scope("s29_sx3"):
+        swap_x(3)
+    with jax.named_scope("s30_r3"):
+        ring(3)
+    with jax.named_scope("s31_q2"):
+        ring_slice(2)
+    with jax.named_scope("s32_sx4"):
+        swap_x(4)
+    with jax.named_scope("s33_q3"):
+        ring_slice(3)
+    with jax.named_scope("s34_r4"):
+        ring(4)
+    with jax.named_scope("s35_q4"):
+        ring_slice(4)
+    with jax.named_scope("s36_sy0"):
         swap_y(0)
-    with jax.named_scope("s28_sx3"):
-        swap_x(3)
-    with jax.named_scope("s29_r2"):
-        ring(2)
-    with jax.named_scope("s30_sx4"):
-        swap_x(4)
-    with jax.named_scope("s31_sx0"):
+    with jax.named_scope("s37_r5"):
+        ring(5)
+    with jax.named_scope("s38_q5"):
+        ring_slice(5)
+    with jax.named_scope("s39_sx0"):
         swap_x(0)
-    with jax.named_scope("s32_r3"):
-        ring(3)
-    with jax.named_scope("s33_r4"):
-        ring(4)
-    with jax.named_scope("s34_r5"):
-        ring(5)
-    with jax.named_scope("s35_r6"):
+    with jax.named_scope("s40_r6"):
         ring(6)
-    with jax.named_scope("s36_r7"):
+    with jax.named_scope("s41_q6"):
+        ring_slice(6)
+    with jax.named_scope("s42_r7"):
         ring(7)
-    cw = cr // NY
-    with jax.named_scope("final"):
-        for h in (0, 1):
-            r = pl.ds(h * half, half)
-            x_arrive(0, h)
-            for q in (0, 1):
-                rq = pl.ds(q * quarter, quarter)
-                arrive(zin.at[h, NZ - 2, rq], zin_sem.at[h, NZ - 2, q])
-            for (lo, hi), v in zip(bounds, summed(0, r)):
-                v = (v + xx[0, r, lo:hi].astype(F32) + zin[h, NZ - 2, :, lo:hi].astype(F32)).astype(BF)
-                if lo == 0:
-                    for i in range(NY):
-                        tsb[2 * i + h, :, 0:cw] = v[:, i * cw : (i + 1) * cw]
-                else:
-                    tsb[2 * y + h, :, cw : cw + sr] = v
+    with jax.named_scope("s43_q7"):
+        ring_slice(7)
+    with jax.named_scope("s44_r8"):
+        ring(8)
+    with jax.named_scope("s45_t"):
+        tensor_send(1)
+    with jax.named_scope("s46_q8"):
+        ring_slice(8)
     me = 2 * y + xh
     with jax.named_scope("tensor_sum"):
-        for yp, xp, i, j in peers:
-            n = cw + sr if i == 0 else cw
-            send(
-                "t0" if i == 0 else "t1", tsb.at[2 * yp + xp, :, pl.ds(0, n)],
-                tsi.at[2 * ((NY - i) % NY) + j, :, pl.ds(0, n)],
-                ts_sem.at[min(i, 1)], {"y": yp, "xh": xp},
-            )
+        tensor_send(0)
         mate_sum, far_sums = tsi.at[1, :, pl.ds(0, cw + sr)], tsi.at[pl.ds(2, 6), :, pl.ds(0, cw)]
         arrive(mate_sum, ts_sem.at[0])
         acc = tsb[me, :, 0:cw].astype(F32) + tsi[1, :, 0:cw].astype(F32)
-        if GR:
-            fin[:, cw : cw + sr] = (
-                tsb[me, :, cw : cw + sr].astype(F32) + tsi[1, :, cw : cw + sr].astype(F32)
-            ).astype(BF)
+        fin[:, cw : cw + sr] = (
+            tsb[me, :, cw : cw + sr].astype(F32) + tsi[1, :, cw : cw + sr].astype(F32)
+        ).astype(BF)
         arrive(far_sums, ts_sem.at[1])
         for i in range(2, 8):
             acc = acc + tsi[i, :, 0:cw].astype(F32)
@@ -385,20 +412,19 @@
             for j in (0, 1):
                 r = pl.ds(j * half, half)
                 out[r, i * cw : (i + 1) * cw] = agi[2 * i + j, :, 0:cw]
-                if GR:
-                    out[r, cr + i * sr : cr + (i + 1) * sr] = agi[2 * i + j, :, cw : cw + sr]
+                out[r, cr + i * sr : cr + (i + 1) * sr] = agi[2 * i + j, :, cw : cw + sr]
     all_sent("z", gath.at[pl.ds(0, 7), 0, :, pl.ds(0, aw)])
     all_sent("x", gath.at[:, 0, :, pl.ds(0, aw)])
     if GA:
         all_sent("y", gath.at[pl.ds(0, 7), :, :, pl.ds(0, 3 * sa)])
         all_sent("y0", gath.at[0, 0, :, pl.ds(0, 3 * sa)])
     all_sent("xx0", part.at[:, 0, :, pl.ds(0, cr)])
-    if GR:
-        all_sent("xx1", part.at[:, 0, :, pl.ds(0, sr)])
-        all_sent("yy", yy)
-    all_sent("zz", zout)
-    for i, (ref, at) in enumerate(moved):
-        all_sent(f"w{i}", at_rows(ref, at))
+    all_sent("xx1", part.at[:, 0, :, pl.ds(0, sr)])
+    all_sent("yy", yy)
+    all_sent("zz0", zout.at[:, :, :, bounds[0]])
+    all_sent("zz1", zout.at[:, :, :, bounds[1]])
+    for i, (ref, n) in enumerate(moved):
+        all_sent(f"w{i}", ref.at[pl.ds(0, n)])
     all_sent("t0", mate_sum)
     all_sent("t1", far_sums)
     all_sent("t2", others)
@@ -436,8 +462,8 @@
             pltpu.VMEM(last, BF),
             pltpu.VMEM(last[1:], BF),
             pltpu.VMEM(last, BF),
-            dma((9,)), dma((14,)), dma((3,)), dma((NZ, 2)), dma((NZ,)), dma((NZ,)),
-            dma((NZ,)), dma((NZ, 2)), dma((2, NZ - 1, 2)), dma((2,)), dma((1,)),
+            dma((9,)), dma((15,)), dma((2,)), dma((NZ, 2)), dma((NZ,)), dma((NZ,)),
+            dma((NZ,)), dma((NZ, 2, 2)), dma((2, NZ - 1, 3)), dma((2,)), dma((1,)),
         ],
         compiler_params=pltpu.CompilerParams(
             collective_id=0, has_side_effects=True, vmem_limit_bytes=62 * 1024 * 1024

time: 87 us -> 81.5 us (0.937); the launches traced: 85.8 us -> 81.4 us
  Pallas kernels: 84.2 us -> 79.7 us
    pallas_call x1, Pallas kernels: 84.2 us -> 79.7 us  [layer(): pl.pallas_call(kernel, out_shape=jax.ShapeDtypeStruct((rows, dim), BF), i...]
where the time goes in v5:
time: 81.5 us; the launch traced here: 81.4 us
  Pallas kernels  79.7 us (98%)
  local copies, waits for them, and re-layouts  1.67 us (2%)
    pallas_call x1, Pallas kernels, layer(): pl.pallas_call(kernel, out_shape=jax.ShapeDtypeStruct((rows, dim), BF), i...  79.7 us
    unnamed x1, local copies, waits for them, and re-layouts  1.67 us

profile of v5, /device:TPU:2, one launch (start us, length us, event | category | flops | bytes accessed | tf_op | source)
XLA Modules:
  0.0 81.4 jit_solution(16184087069140148501)
XLA Ops:
  0.0 79.7 %shard_map.91 = bf16[64,2048]{1,0:T(8,128)(2,1)} custom-call(bf16[64,2048]{1,0:T(8,128)(2,1)} %tokens.1, s32[6,2048]{1,0:T(8,128)} %bitcast.16, f32[6,2048]{1,0:T(8,128)} %bitcast.17, bf16[352,2048]{1,0:T(8,128)(2,1)} %bitcast.11, bf16[352,2048]{1,0:T(8,128)(2,1)} %bitcast.12, bf16[352,2048]{1,0:T(8,128)(2,1)} %bitcast.13, bf16[352,2048]{1,0:T(8,128)(2,1)} %bitcast.14, ...), custom_call_target="tpu_custom_call" | custom-call | tf_op jit(solution)/shard_map/pallas_call | solution.py:440
  79.7 1.7 %copy.11 = bf16[64,2048]{1,0:T(8,128)(2,1)} copy(bf16[64,2048]{1,0:T(8,128)(2,1)} %shard_map.91) | data formatting | bytes 524288

commit v6 on v5

--- a/solution.py
+++ b/solution.py
@@ -13,6 +13,7 @@
 BF, F32 = jnp.bfloat16, jnp.float32
 GA, GR = 512, 512
 DC = 512
+NP = 2
 NT_DIMS = (((1,), (1,)), ((), ()))
 
 
@@ -199,9 +200,16 @@
                     "yy", part.at[slot, :, :, pl.ds(cr + i * sr, sr)], yy.at[slot, NY - i - 1],
                     yr_sem.at[slot], {"y": yat[i]},
                 )
+        swap_common(k, True)
+
+    def swap_common(k, soon):
         for slot in slots(k):
             for h, dev in sides:
-                x_send(slot, h, dev, 0)
+                if soon == (k in (0, 4) or (h == 0) == (OFFSETS[slot] < 0)):
+                    x_send(slot, h, dev, 0)
+
+    def swap_late(k):
+        swap_common(k, False)
 
     def sliced(slot, b, r):
         v = part[slot, b, r, cr:rw].astype(F32)
@@ -216,9 +224,8 @@
             for h, dev in sides:
                 x_send(slot, h, dev, 1)
 
-    def ring_step(s, which, r_in, r_full, sem, h, up):
+    def ring_step(s, which, cols, r_in, r_full, sem, h, up):
         slot = SLOT[(-s if up else s) % NZ]
-        cols = bounds[which]
         v = xx[slot, r_full, cols].astype(F32)
         v = v + (sliced(slot, xl, r_full) if which else part[slot, xl, r_full, cols].astype(F32))
         if s > 1:
@@ -239,21 +246,24 @@
             slot = SLOT[(-s if up else s) % NZ]
             x_at = xx.at[slot, pl.ds(h * half, half), bounds[0]]
             arrive(x_at, xx_sem.at[slot, h, 0])
-        for q in (0, 1):
+        n = cr // NP
+        for q, p in [(q, p) for q in (0, 1) for p in range(NP)]:
             for h, up in directions:
                 v = ring_step(
-                    s, 0, pl.ds(q * quarter, quarter), pl.ds(h * half + q * quarter, quarter),
-                    lambda i: zin_sem.at[h, i, q], h, up,
+                    s, 0, pl.ds(p * n, n), pl.ds(q * quarter, quarter),
+                    pl.ds(h * half + q * quarter, quarter),
+                    lambda i: zin_sem.at[h, i, q * NP + p], h, up,
                 )
-                for i in range(NY if s == NZ else 0):
-                    tsb[2 * i + h, q * quarter : (q + 1) * quarter, 0:cw] = v[:, i * cw : (i + 1) * cw]
+                for i in range(NY // NP if s == NZ else 0):
+                    at = 2 * (p * NY // NP + i) + h
+                    tsb[at, q * quarter : (q + 1) * quarter, 0:cw] = v[:, i * cw : (i + 1) * cw]
 
     def ring_slice(s):
         for h, up in directions:
             slot = SLOT[(-s if up else s) % NZ]
             full = pl.ds(h * half, half)
             arrive(xx.at[slot, full, bounds[1]], xx_sem.at[slot, h, 1])
-            v = ring_step(s, 1, pl.ds(0, half), full, lambda i: zin_sem.at[h, i, 2], h, up)
+            v = ring_step(s, 1, bounds[1], pl.ds(0, half), full, lambda i: zin_sem.at[h, i, 2 * NP], h, up)
             if s == NZ:
                 tsb[2 * y + h, :, cw : cw + sr] = v
 
@@ -359,35 +369,41 @@
         ring(3)
     with jax.named_scope("s31_q2"):
         ring_slice(2)
-    with jax.named_scope("s32_sx4"):
+    with jax.named_scope("s32_xl3"):
+        swap_late(3)
+    with jax.named_scope("s33_sx4"):
         swap_x(4)
-    with jax.named_scope("s33_q3"):
-        ring_slice(3)
     with jax.named_scope("s34_r4"):
         ring(4)
-    with jax.named_scope("s35_q4"):
-        ring_slice(4)
-    with jax.named_scope("s36_sy0"):
-        swap_y(0)
+    with jax.named_scope("s35_q3"):
+        ring_slice(3)
+    with jax.named_scope("s36_xl2"):
+        swap_late(2)
     with jax.named_scope("s37_r5"):
         ring(5)
-    with jax.named_scope("s38_q5"):
+    with jax.named_scope("s38_q4"):
+        ring_slice(4)
+    with jax.named_scope("s39_xl1"):
+        swap_late(1)
+    with jax.named_scope("s40_sy0"):
+        swap_y(0)
+    with jax.named_scope("s41_r6"):
+        ring(6)
+    with jax.named_scope("s42_q5"):
         ring_slice(5)
-    with jax.named_scope("s39_sx0"):
+    with jax.named_scope("s43_sx0"):
         swap_x(0)
-    with jax.named_scope("s40_r6"):
-        ring(6)
-    with jax.named_scope("s41_q6"):
+    with jax.named_scope("s44_r7"):
+        ring(7)
+    with jax.named_scope("s45_q6"):
         ring_slice(6)
-    with jax.named_scope("s42_r7"):
-        ring(7)
-    with jax.named_scope("s43_q7"):
+    with jax.named_scope("s46_q7"):
         ring_slice(7)
-    with jax.named_scope("s44_r8"):
+    with jax.named_scope("s47_r8"):
         ring(8)
-    with jax.named_scope("s45_t"):
+    with jax.named_scope("s48_t"):
         tensor_send(1)
-    with jax.named_scope("s46_q8"):
+    with jax.named_scope("s49_q8"):
         ring_slice(8)
     me = 2 * y + xh
     with jax.named_scope("tensor_sum"):
@@ -463,7 +479,7 @@
             pltpu.VMEM(last[1:], BF),
             pltpu.VMEM(last, BF),
             dma((9,)), dma((15,)), dma((2,)), dma((NZ, 2)), dma((NZ,)), dma((NZ,)),
-            dma((NZ,)), dma((NZ, 2, 2)), dma((2, NZ - 1, 3)), dma((2,)), dma((1,)),
+            dma((NZ,)), dma((NZ, 2, 2)), dma((2, NZ - 1, 2 * NP + 1)), dma((2,)), dma((1,)),
         ],
         compiler_params=pltpu.CompilerParams(
             collective_id=0, has_side_effects=True, vmem_limit_bytes=62 * 1024 * 1024

time: 81.5 us -> 79.4 us (0.974)
  Pallas kernels: 79.7 us -> 77.5 us
    pallas_call x1, Pallas kernels: 79.7 us -> 77.5 us  [layer(): pl.pallas_call(kernel, out_shape=jax.ShapeDtypeStruct((rows, dim), BF), i...]
where the time goes in v6:
time: 79.4 us; the launch traced here: 79.1 us
  Pallas kernels  77.5 us (98%)
  local copies, waits for them, and re-layouts  1.67 us (2%)
    pallas_call x1, Pallas kernels, layer(): pl.pallas_call(kernel, out_shape=jax.ShapeDtypeStruct((rows, dim), BF), i...  77.5 us
    unnamed x1, local copies, waits for them, and re-layouts  1.67 us

profile of v6, /device:TPU:2, one launch (start us, length us, event | category | flops | bytes accessed | tf_op | source)
XLA Modules:
  0.0 79.1 jit_solution(14761057153429811729)
XLA Ops:
  0.0 77.5 %shard_map.91 = bf16[64,2048]{1,0:T(8,128)(2,1)} custom-call(bf16[64,2048]{1,0:T(8,128)(2,1)} %tokens.1, s32[6,2048]{1,0:T(8,128)} %bitcast.16, f32[6,2048]{1,0:T(8,128)} %bitcast.17, bf16[352,2048]{1,0:T(8,128)(2,1)} %bitcast.11, bf16[352,2048]{1,0:T(8,128)(2,1)} %bitcast.12, bf16[352,2048]{1,0:T(8,128)(2,1)} %bitcast.13, bf16[352,2048]{1,0:T(8,128)(2,1)} %bitcast.14, ...), custom_call_target="tpu_custom_call" | custom-call | tf_op jit(solution)/shard_map/pallas_call | solution.py:456
  77.5 1.7 %copy.11 = bf16[64,2048]{1,0:T(8,128)(2,1)} copy(bf16[64,2048]{1,0:T(8,128)(2,1)} %shard_map.91) | data formatting | bytes 524288

commit v7 on v6

--- a/solution.py
+++ b/solution.py
@@ -343,10 +343,10 @@
         swap_x(1)
     with jax.named_scope("s18_gx4"):
         gather_x(4)
-    with jax.named_scope("s19_gy3"):
+    with jax.named_scope("s19_r1"):
+        ring(1)
+    with jax.named_scope("s20_gy3"):
         gather_y(3)
-    with jax.named_scope("s20_r1"):
-        ring(1)
     with jax.named_scope("s21_c3"):
         compute(3)
     with jax.named_scope("s22_sy3"):

time: 79.4 us -> 79.6 us (level)
  no operation moved by 1% of the time
where the time goes in v7:
time: 79.6 us; the launch traced here: 78.6 us
  Pallas kernels  76.9 us (97%)
  local copies, waits for them, and re-layouts  1.67 us (2%)
    pallas_call x1, Pallas kernels, layer(): pl.pallas_call(kernel, out_shape=jax.ShapeDtypeStruct((rows, dim), BF), i...  76.9 us
    unnamed x1, local copies, waits for them, and re-layouts  1.67 us

profile of v7, /device:TPU:2, one launch (start us, length us, event | category | flops | bytes accessed | tf_op | source)
XLA Modules:
  0.0 78.6 jit_solution(11862565762145454660)
XLA Ops:
  0.0 76.9 %shard_map.91 = bf16[64,2048]{1,0:T(8,128)(2,1)} custom-call(bf16[64,2048]{1,0:T(8,128)(2,1)} %tokens.1, s32[6,2048]{1,0:T(8,128)} %bitcast.16, f32[6,2048]{1,0:T(8,128)} %bitcast.17, bf16[352,2048]{1,0:T(8,128)(2,1)} %bitcast.11, bf16[352,2048]{1,0:T(8,128)(2,1)} %bitcast.12, bf16[352,2048]{1,0:T(8,128)(2,1)} %bitcast.13, bf16[352,2048]{1,0:T(8,128)(2,1)} %bitcast.14, ...), custom_call_target="tpu_custom_call" | custom-call | tf_op jit(solution)/shard_map/pallas_call | solution.py:456
  77.0 1.7 %copy.11 = bf16[64,2048]{1,0:T(8,128)(2,1)} copy(bf16[64,2048]{1,0:T(8,128)(2,1)} %shard_map.91) | data formatting | bytes 524288
